TPU v7x, 32 devices: a whole 2x2x4 slice. The times are simulated.
32 devices in a mesh: replica: 16 (over z, x, core), spatial: 2 (over y).
Axes of the slice: x: 2, y: 2, z: 4, core: 2. Of those that a mesh axis runs over, the one named last changes fastest.
Arguments:
- grads: bfloat16 [16, 2, 852992], P('replica', 'spatial'), may hold values from -6 to 6
- master: float32 [852992], P(('replica', 'spatial')), may hold values from -0.06 to 0.06
- velocity: float32 [852992], P(('replica', 'spatial')), may hold values from -0.3 to 0.3
- layer_offsets: int32 [6], replicated, may hold values from 0 to 852736, as said below
- layer_sizes: int32 [6], replicated, may hold values from 256 to 589824
- lars_skip: int32 [6], replicated, may hold values from 0 to 1
Outputs:
- new_weights: bfloat16 [852992], replicated
- new_master: float32 [852992], P(('replica', 'spatial'))
- new_velocity: float32 [852992], P(('replica', 'spatial'))
Inputs may be any that keep to these rules, and one draw needn't show every extreme that they name: layer_offsets, layer_sizes and lars_skip describe the six tensors (a 256 x 1024 convolution, a 256 x 256 x 9 convolution, and two gains and two shifts of 256 entries) laid end to end in some order without gaps, the last of them always a gain or a shift; lars_skip is 1 exactly for the gains and shifts.
All inputs are finite; a program needn't handle non-finite values.
Results may differ from a plain program's by a relative error of at most 0.001.
Values may be sent and summed in bfloat16 or wider, within the bound.
A program may use at most 64 MiB of HBM per device.

v0:
```python
import functools
import math

import jax
import jax.numpy as jnp
from jax import lax
from jax.experimental import pallas as pl
from jax.experimental.pallas import tpu as pltpu
from jax.sharding import PartitionSpec as P

MESH = pl.DeviceIdType.MESH
TILE = 1024


def kernel(
    plan,
    grads_ref,
    m_ref,
    v_ref,
    offsets_ref,
    sizes_ref,
    skip_ref,
    ags,
    nmw,
    nvw,
    m_in,
    v_in,
    gin,
    packed,
    recv1,
    part,
    recv2,
    mv,
    halo,
    grad_buf,
    wrow,
    stats,
    in_sem,
    mv_sem,
    send1,
    got1,
    send2,
    got2,
    halo_sem,
    send3,
    got3,
    send4,
    got4,
):
    n_out, n_a, n_spa, shard, step, span, layers = plan
    plane = n_a * 2 * n_spa
    n = n_out * plane
    chunk = (plane - 1) * step + span
    rows = span * 8
    r = lax.axis_index("replica")
    s = lax.axis_index("spatial")
    d = r * n_spa + s
    z = d // plane
    p = d % plane
    a = p // (2 * n_spa)
    c = (p // n_spa) % 2
    base = d * (step * TILE)
    off = d * (shard - step * TILE)

    def dev(flat):
        return (flat // n_spa, flat % n_spa)

    barrier = pltpu.get_barrier_semaphore()

    def load(zt):
        start = pl.multiple_of(zt * (plane * step * TILE), TILE)
        return pltpu.make_async_copy(
            grads_ref.at[0, :, pl.ds(start, chunk * TILE)], gin.at[zt], in_sem.at[zt]
        )

    for k in range(1, n_out + 1):
        load((z + k) % n_out).start()
    mv_loads = [
        pltpu.make_async_copy(ref, buf, mv_sem.at[j])
        for j, (ref, buf) in enumerate(((m_ref, m_in), (v_ref, v_in)))
    ]
    for copy in mv_loads:
        copy.start()

    @pl.loop(1, n, unroll=True)
    def _(q):
        pl.semaphore_signal(barrier, inc=1, device_id=dev((d + q) % n), device_id_type=MESH)

    group = max(g for g in range(1, 33) if chunk % g == 0)

    def pack(zt):
        load(zt).wait()

        @pl.loop(0, chunk // group)
        def _(i):
            at = pl.multiple_of(i * (group * TILE), group * TILE)
            v = gin[zt, :, pl.ds(at, group * TILE)].astype(jnp.float32)
            packed[zt, pl.ds(i * group, group)] = v.reshape(group, 8, 128).astype(jnp.bfloat16)

    def copy1(zt, src, dst):
        return pltpu.make_async_remote_copy(
            src_ref=packed.at[zt, pl.ds(dst * step, span)],
            dst_ref=recv1.at[zt, src],
            send_sem=send1,
            recv_sem=got1.at[zt, src],
            device_id=dev(z * plane + dst),
            device_id_type=MESH,
        )

    for k in range(1, n_out + 1):
        zt = (z + k) % n_out
        pack(zt)
        if k == 1:
            pl.semaphore_wait(barrier, n - 1)

        @pl.loop(1, plane, unroll=True)
        def _(q):
            copy1(zt, p, (p + q) % plane).start()

    lane = lax.broadcasted_iota(jnp.int32, (rows, 128), 1)
    shift_l = off % 128
    shift_r = off // 128
    whole = step * TILE
    for j, ref in enumerate((m_in, v_in)):
        mv_loads[j].wait()
        edge = jnp.pad(ref[pl.ds(whole, shard - whole)], (0, 128 - (shard - whole)))
        edge = jnp.broadcast_to(edge.reshape(1, 128), (8, 128))
        x = jnp.concatenate([ref[pl.ds(0, whole)].reshape(step * 8, 128), edge], 0)
        x = pltpu.roll(x, shift_l, 1)
        x = jnp.where(lane < shift_l, pltpu.roll(x, 1, 0), x)
        x = pltpu.roll(x, shift_r, 0)
        mv[:, j] = x.reshape(span, 8, 128)
    halo_copy = pltpu.make_async_remote_copy(
        src_ref=mv.at[span - 1],
        dst_ref=halo,
        send_sem=halo_sem.at[0],
        recv_sem=halo_sem.at[1],
        device_id=dev((d + 1) % n),
        device_id_type=MESH,
    )
    halo_copy.start()

    place = lax.broadcasted_iota(jnp.int32, (8, 128), 0) * 128 + lax.broadcasted_iota(
        jnp.int32, (8, 128), 1
    )
    low = [offsets_ref[l] - base for l in range(layers)]
    high = [offsets_ref[l] + sizes_ref[l] - base for l in range(layers)]
    own_low = [jnp.maximum(x, off) for x in low]
    own_high = [jnp.minimum(x, off + shard) for x in high]
    lane1 = lax.broadcasted_iota(jnp.int32, (1, 128), 1)

    def squares(value, first):
        def add(t, accs):
            pos = place + t * TILE
            x = value(t)
            x = x * x
            return tuple(
                acc + jnp.where((pos >= lo) & (pos < hi), x, 0.0)
                for acc, lo, hi in zip(accs, own_low, own_high)
            )

        accs = lax.fori_loop(
            0, span, add, tuple(jnp.zeros((8, 128), jnp.float32) for _ in range(layers))
        )
        row = jnp.zeros((1, 128), jnp.float32)
        for l, acc in enumerate(accs):
            row = jnp.where(lane1 == first + l, jnp.sum(acc, axis=(0, 1), keepdims=True), row)
        return row

    wrow[...] = squares(lambda t: mv[t, 0], 0)

    def copy2(zt, src):
        return pltpu.make_async_remote_copy(
            src_ref=part.at[zt],
            dst_ref=recv2.at[src],
            send_sem=send2,
            recv_sem=got2.at[src],
            device_id=dev(zt * plane + p),
            device_id_type=MESH,
        )

    for k in range(1, n_out + 1):
        zt = (z + k) % n_out

        @pl.loop(1, plane)
        def _(q):
            copy1(zt, (p + q) % plane, p).wait_recv()

        @pl.loop(0, span)
        def _(t):
            acc = packed[zt, p * step + t].astype(jnp.float32)
            for q in range(1, plane):
                acc = acc + recv1[zt, (p + q) % plane, t].astype(jnp.float32)
            part[zt, t] = acc

        if k < n_out:
            copy2(zt, z).start()

    halo_copy.wait()
    for j in range(2):
        mv[0, j] = jnp.where(place < off, halo[j], mv[0, j])

    @pl.loop(1, n_out)
    def _(k):
        copy2(z, (z + k) % n_out).wait_recv()

    @pl.loop(0, span)
    def _(t):
        acc = part[z, t]
        for k in range(1, n_out):
            acc = acc + recv2[(z + k) % n_out, t]
        grad_buf[t] = acc / n

    stats[d] = squares(lambda t: grad_buf[t], layers) + wrow[...]

    def copy3(src, dst):
        return pltpu.make_async_remote_copy(
            src_ref=stats.at[src],
            dst_ref=stats.at[src],
            send_sem=send3,
            recv_sem=got3.at[src],
            device_id=dev(dst),
            device_id_type=MESH,
        )

    @pl.loop(1, n, unroll=True)
    def _(q):
        copy3(d, (d + q) % n).start()

    @pl.loop(1, n, unroll=True)
    def _(q):
        copy3((d + q) % n, d).wait_recv()

    total = jnp.sum(stats[...], axis=0)
    trust, decay = [], []
    for l in range(layers):
        wsq = jnp.sum(jnp.where(lane1 == l, total, 0.0), axis=(0, 1), keepdims=True)
        gsq = jnp.sum(jnp.where(lane1 == layers + l, total, 0.0), axis=(0, 1), keepdims=True)
        wnorm = jnp.sqrt(jnp.broadcast_to(wsq, (8, 128)))
        gnorm = jnp.sqrt(jnp.broadcast_to(gsq, (8, 128)))
        skipped = skip_ref[l].astype(jnp.float32)
        ratio = 0.02 * wnorm / (gnorm + 0.001 * wnorm + 1e-06)
        trust.append(skipped + (1.0 - skipped) * ratio)
        decay.append((1.0 - skipped) * 0.001)

    @pl.loop(0, span)
    def _(t):
        pos = place + t * TILE
        trust_pos = jnp.zeros((8, 128), jnp.float32)
        decay_pos = jnp.zeros((8, 128), jnp.float32)
        for l in range(layers):
            inside = (pos >= low[l]) & (pos < high[l])
            trust_pos = jnp.where(inside, trust[l], trust_pos)
            decay_pos = jnp.where(inside, decay[l], decay_pos)
        m = mv[t, 0]
        nv = 0.9 * mv[t, 1] + 8.0 * trust_pos * (grad_buf[t] + decay_pos * m)
        nm = m - nv
        nvw[t] = nv
        nmw[t] = nm
        ags[d, t] = nm.astype(jnp.bfloat16)

    def copy4(block, dst):
        return pltpu.make_async_remote_copy(
            src_ref=ags.at[block],
            dst_ref=ags.at[block],
            send_sem=send4,
            recv_sem=got4.at[block],
            device_id=dev(dst),
            device_id_type=MESH,
        )

    n_same = plane // 2
    me_same = a * n_spa + s
    partner = z * plane + a * (2 * n_spa) + (1 - c) * n_spa + s

    def same(index, core):
        return (index // n_spa) * (2 * n_spa) + core * n_spa + index % n_spa

    def to_plane(zz):
        block = zz * plane + p

        @pl.loop(1, n_same)
        def _(q):
            peer = (me_same + q) % n_same
            copy4(block, z * plane + same(peer, c)).start()

    def to_partner(zz, index):
        block = zz * plane + same(index, c)
        copy4(block, partner).start()

    @pl.loop(1, n_out)
    def _(k):
        zz = (z + k) % n_out
        copy4(d, zz * plane + p).start()

    to_plane(z)
    to_partner(z, me_same)

    @pl.loop(1, n_out)
    def _(k):
        zz = (z + k) % n_out
        copy4(zz * plane + p, d).wait_recv()
        to_plane(zz)
        to_partner(zz, me_same)

    @pl.loop(0, n_out)
    def _(k):
        zz = (z + k) % n_out

        @pl.loop(1, n_same)
        def _(q):
            peer = (me_same + q) % n_same
            copy4(zz * plane + same(peer, c), d).wait_recv()
            to_partner(zz, peer)

    @pl.loop(0, n_out)
    def _(k):
        zz = (z + k) % n_out

        @pl.loop(0, n_same)
        def _(q):
            peer = (me_same + q) % n_same
            block = zz * plane + same(peer, 1 - c)
            copy4(block, d).wait_recv()

    for ref, sem in (
        (recv1.at[:, pl.ds(0, plane - 1)], send1),
        (recv2.at[pl.ds(0, n_out - 1)], send2),
        (stats.at[pl.ds(0, n - 1)], send3),
        (ags.at[pl.ds(0, n - 1)], send4),
    ):
        pltpu.make_async_copy(ref, ref, sem).wait()


def finish(plan, ags, nmw, nvw, out_ref, nm_ref, nv_ref, nm_out, nv_out, out_sem, own_sem):
    n, n_spa, shard, step, span = plan
    rows = span * 8
    whole = step * TILE
    copies = [
        pltpu.make_async_copy(
            ags.at[b, pl.ds(0, step)], out_ref.at[pl.ds(b * step, step)], out_sem.at[b]
        )
        for b in range(n)
    ]
    copies.append(
        pltpu.make_async_copy(
            ags.at[n - 1, pl.ds(step, span - step)],
            out_ref.at[pl.ds(n * step, span - step)],
            out_sem.at[n],
        )
    )
    for copy in copies:
        copy.start()
    d = lax.axis_index("replica") * n_spa + lax.axis_index("spatial")
    off = d * (shard - whole)
    shift_l = off % 128
    shift_r = off // 128
    back_l = 128 - shift_l
    lane = lax.broadcasted_iota(jnp.int32, (rows, 128), 1)
    for j, (src, buf, ref) in enumerate(((nmw, nm_out, nm_ref), (nvw, nv_out, nv_ref))):
        x = src[...].reshape(rows, 128)
        x = pltpu.roll(x, (rows - shift_r) % rows, 0)
        x = pltpu.roll(x, back_l % 128, 1)
        x = jnp.where(lane < back_l, x, pltpu.roll(x, rows - 1, 0))
        buf[pl.ds(0, whole)] = x[: step * 8].reshape(whole)
        buf[pl.ds(whole, shard - whole)] = x[step * 8, : shard - whole].reshape(shard - whole)
        copy = pltpu.make_async_copy(buf, ref, own_sem.at[j])
        copy.start()
        copies.append(copy)
    for copy in copies:
        copy.wait()


def windowed(n_rep, n_spa, grads, master, velocity, layer_offsets, layer_sizes, lars_skip):
    shard = master.shape[0]
    params = grads.shape[2]
    layers = layer_offsets.shape[0]
    n_in = math.isqrt(n_rep)
    n_out, n_a = n_rep // n_in, n_in // 2
    n = n_rep * n_spa
    plane = n_in * n_spa
    step = shard // TILE
    span = params // TILE - (n - 1) * step
    chunk = (plane - 1) * step + span
    tiles = params // TILE
    plan = (n_out, n_a, n_spa, shard, step, span, layers)
    vmem = pl.BlockSpec(memory_space=pltpu.VMEM)
    smem = pl.BlockSpec(memory_space=pltpu.SMEM)
    anywhere = pl.BlockSpec(memory_space=pltpu.HBM)
    f32, bf16 = jnp.float32, jnp.bfloat16
    dma = pltpu.SemaphoreType.DMA
    ags, nmw, nvw = pl.pallas_call(
        functools.partial(kernel, plan),
        out_shape=(
            pltpu.VMEM((n, span, 8, 128), bf16),
            pltpu.VMEM((span, 8, 128), f32),
            pltpu.VMEM((span, 8, 128), f32),
        ),
        in_specs=[anywhere, anywhere, anywhere, smem, smem, smem],
        out_specs=(vmem, vmem, vmem),
        scratch_shapes=[
            pltpu.VMEM((shard,), f32),
            pltpu.VMEM((shard,), f32),
            pltpu.VMEM((n_out, 1, chunk * TILE), bf16),
            pltpu.VMEM((n_out, chunk, 8, 128), bf16),
            pltpu.VMEM((n_out, plane, span, 8, 128), bf16),
            pltpu.VMEM((n_out, span, 8, 128), f32),
            pltpu.VMEM((n_out, span, 8, 128), f32),
            pltpu.VMEM((span, 2, 8, 128), f32),
            pltpu.VMEM((2, 8, 128), f32),
            pltpu.VMEM((span, 8, 128), f32),
            pltpu.VMEM((1, 128), f32),
            pltpu.VMEM((n, 1, 128), f32),
            dma((n_out,)),
            dma((2,)),
            dma(()),
            dma((n_out, plane)),
            dma(()),
            dma((n_out,)),
            dma((2,)),
            dma(()),
            dma((n,)),
            dma(()),
            dma((n,)),
        ],
        compiler_params=pltpu.CompilerParams(
            collective_id=0, has_side_effects=True, vmem_limit_bytes=61 * 2**20
        ),
    )(grads, master, velocity, layer_offsets, layer_sizes, lars_skip)
    weights, nm, nv = pl.pallas_call(
        functools.partial(finish, (n, n_spa, shard, step, span)),
        out_shape=(
            jax.ShapeDtypeStruct((tiles, 8, 128), bf16),
            jax.ShapeDtypeStruct((shard,), f32),
            jax.ShapeDtypeStruct((shard,), f32),
        ),
        in_specs=[vmem, vmem, vmem],
        out_specs=(anywhere, anywhere, anywhere),
        scratch_shapes=[
            pltpu.VMEM((shard,), f32),
            pltpu.VMEM((shard,), f32),
            dma((n + 1,)),
            dma((2,)),
        ],
        compiler_params=pltpu.CompilerParams(vmem_limit_bytes=16 * 2**20),
    )(ags, nmw, nvw)
    return weights.reshape(params), nm, nv


def tiled(n_rep, n_spa, params):
    n = n_rep * n_spa
    shard = params // n
    n_in = math.isqrt(n_rep)
    rest = shard % TILE
    return (
        n_in * n_in == n_rep
        and n_in % 2 == 0
        and params % TILE == 0
        and shard >= TILE
        and 0 < n * rest <= TILE
        and rest <= 128
    )


def step_fn(n_rep, n_spa, grads, *rest):
    if tiled(n_rep, n_spa, grads.shape[2]):
        return windowed(n_rep, n_spa, grads, *rest)
    return shards(grads, *rest)


def shards(grads, master, velocity, layer_offsets, layer_sizes, lars_skip):
    n_rep = lax.axis_size("replica")
    n_spa = lax.axis_size("spatial")
    shard = master.shape[0]
    position = lax.axis_index(("replica", "spatial")) * shard + jnp.arange(shard, dtype=jnp.int32)
    inside = (position[None, :] >= layer_offsets[:, None]) & (
        position[None, :] < (layer_offsets + layer_sizes)[:, None]
    )
    onehot = inside.astype(jnp.float32)
    received = lax.all_to_all(
        grads[0, 0].reshape(n_rep, n_spa * shard),
        "replica",
        split_axis=0,
        concat_axis=0,
        tiled=True,
    )
    first = jnp.sum(received.astype(jnp.float32), axis=0)
    summed = lax.psum_scatter(
        first.reshape(n_spa, shard), "spatial", scatter_dimension=0, tiled=True
    )
    grad = summed.reshape(shard) / (n_rep * n_spa)
    gsq_local = jnp.dot(onehot, grad * grad, precision=lax.Precision.HIGHEST)
    wsq_local = jnp.dot(onehot, master * master, precision=lax.Precision.HIGHEST)
    wsq, gsq = lax.psum((wsq_local, gsq_local), ("replica", "spatial"))
    wnorm = jnp.sqrt(wsq)
    gnorm = jnp.sqrt(gsq)
    skipped = lars_skip.astype(jnp.float32)
    ratio = 0.02 * wnorm / (gnorm + 0.001 * wnorm + 1e-06)
    trust = skipped + (1.0 - skipped) * ratio
    decay = (1.0 - skipped) * 0.001
    trust_pos = jnp.dot(trust, onehot, precision=lax.Precision.HIGHEST)
    decay_pos = jnp.dot(decay, onehot, precision=lax.Precision.HIGHEST)
    new_velocity = 0.9 * velocity + 8.0 * trust_pos * (grad + decay_pos * master)
    new_master = master - new_velocity
    new_weights = lax.all_gather(
        new_master.astype(jnp.bfloat16), ("replica", "spatial"), axis=0, tiled=True
    )
    return (new_weights, new_master, new_velocity)


def solution(mesh):
    return jax.shard_map(
        functools.partial(step_fn, mesh.shape["replica"], mesh.shape["spatial"]),
        mesh=mesh,
        in_specs=(
            P("replica", "spatial", None),
            P(("replica", "spatial")),
            P(("replica", "spatial")),
            P(),
            P(),
            P(),
        ),
        out_specs=(P(), P(("replica", "spatial")), P(("replica", "spatial"))),
        check_vma=False,
    )
```

profile of v0, /device:TPU:0, one launch (start us, length us, event | category | flops | bytes accessed | tf_op | source)
XLA Modules:
  0.0 52.8 jit_solution(9287251010495428475)
XLA Ops:
  0.6 50.6 %shard_map.85 = (bf16[32,27,8,128]{3,2,1,0:T(8,128)(2,1)S(1)}, f32[27,8,128]{2,1,0:T(8,128)S(1)}, f32[27,8,128]{2,1,0:T(8,128)S(1)}) custom-call(bf16[1,1,852992]{2,1,0:T(2,128)(2,1)} %grads_ref.1, f32[26656]{0:T(1024)} %m_ref.1, f32[26656]{0:T(1024)} %v_ref.1, s32[6]{0:T(128)} %offsets_ref.1, s32[6]{0:T(128)} %sizes_ref.1, s32[6]{0:T(128)} %skip_ref.1), custom_call_target="tpu_custom_call" | custom-call | tf_op jit(solution)/shard_map/pallas_call | solution.py:392
  51.2 1.6 %shard_map.86 = (bf16[833,8,128]{2,1,0:T(8,128)(2,1)}, f32[26656]{0:T(1024)}, f32[26656]{0:T(1024)}) custom-call(bf16[32,27,8,128]{3,2,1,0:T(8,128)(2,1)S(1)} %get-tuple-element.9.ags, f32[27,8,128]{2,1,0:T(8,128)S(1)} %get-tuple-element.10.nmw, f32[27,8,128]{2,1,0:T(8,128)S(1)} %get-tuple-element.11.nvw), custom_call_target="tpu_custom_call" | custom-call | tf_op jit(solution)/shard_map/pallas_call | solution.py:430
where the time goes:
time: 53 us; the launch traced here: 52.8 us
  Pallas kernels  52.2 us (98%)
  between operations  0.64 us (1%)
    pallas_call x1, Pallas kernels, windowed(): pl.pallas_call(functools.partial(kernel, plan), out_shape=(pltpu.VMEM((n,...  50.6 us
    pallas_call x1, Pallas kernels, windowed(): pl.pallas_call(functools.partial(finish, (n, n_spa, shard, step, span)),...  1.57 us

commit v1 on v0

--- a/solution.py
+++ b/solution.py
@@ -1,5 +1,4 @@
 import functools
-import math
 
 import jax
 import jax.numpy as jnp
@@ -10,6 +9,16 @@
 
 MESH = pl.DeviceIdType.MESH
 TILE = 1024
+AHEAD = 2
+
+
+def flip(i, k):
+    out, bit = 0, 1
+    while bit <= k:
+        b = (i // bit) % 2
+        out = out + bit * (1 - 2 * b) * ((k // bit) % 2)
+        bit *= 2
+    return i + out
 
 
 def kernel(
@@ -27,9 +36,14 @@
     v_in,
     gin,
     packed,
-    recv1,
+    r1x,
+    r1y,
+    sx,
+    sy,
+    r2x,
+    r2y,
     part,
-    recv2,
+    recv3,
     mv,
     halo,
     grad_buf,
@@ -37,33 +51,47 @@
     stats,
     in_sem,
     mv_sem,
-    send1,
-    got1,
-    send2,
-    got2,
-    halo_sem,
+    ready,
+    send1x,
+    got1x,
+    send1y,
+    got1y,
+    send2x,
+    got2x,
+    send2y,
+    got2y,
     send3,
     got3,
+    halo_sem,
+    send_s,
+    got_s,
     send4,
     got4,
 ):
-    n_out, n_a, n_spa, shard, step, span, layers = plan
-    plane = n_a * 2 * n_spa
+    n_out, shard, step, span, layers = plan
+    plane = 8
     n = n_out * plane
     chunk = (plane - 1) * step + span
     rows = span * 8
+    hx = (span + 1) // 2
+    hy = span - hx
+    wx = step + 2 * hx - span
+    gap = wx - hx
     r = lax.axis_index("replica")
-    s = lax.axis_index("spatial")
-    d = r * n_spa + s
+    y = lax.axis_index("spatial")
+    d = r * 2 + y
     z = d // plane
     p = d % plane
-    a = p // (2 * n_spa)
-    c = (p // n_spa) % 2
+    x = p // 4
+    c = (p // 2) % 2
     base = d * (step * TILE)
     off = d * (shard - step * TILE)
 
     def dev(flat):
-        return (flat // n_spa, flat % n_spa)
+        return (flat // 2, flat % 2)
+
+    def at(zz, xx, cc, yy):
+        return ((zz * 2 + xx) * 2 + cc, yy)
 
     barrier = pltpu.get_barrier_semaphore()
 
@@ -73,8 +101,9 @@
             grads_ref.at[0, :, pl.ds(start, chunk * TILE)], gin.at[zt], in_sem.at[zt]
         )
 
-    for k in range(1, n_out + 1):
-        load((z + k) % n_out).start()
+    order = [(z + k) % n_out for k in range(1, n_out + 1)]
+    for zt in order:
+        load(zt).start()
     mv_loads = [
         pltpu.make_async_copy(ref, buf, mv_sem.at[j])
         for j, (ref, buf) in enumerate(((m_ref, m_in), (v_ref, v_in)))
@@ -82,9 +111,28 @@
     for copy in mv_loads:
         copy.start()
 
-    @pl.loop(1, n, unroll=True)
-    def _(q):
-        pl.semaphore_signal(barrier, inc=1, device_id=dev((d + q) % n), device_id_type=MESH)
+    def signal(sem, device):
+        pl.semaphore_signal(sem, inc=1, device_id=device, device_id_type=MESH)
+
+    def signal_z(sem):
+        @pl.when(z > 0)
+        def _():
+            signal(sem, at(z - 1, x, c, y))
+
+        @pl.when(z < n_out - 1)
+        def _():
+            signal(sem, at(z + 1, x, c, y))
+
+    n_z = jnp.where(z > 0, 1, 0) + jnp.where(z < n_out - 1, 1, 0)
+    for device in (
+        at(z, x, 1 - c, y),
+        at(z, 1 - x, c, y),
+        at(z, x, c, 1 - y),
+        at(z, 1 - x, 1 - c, y),
+        at(z, x, 1 - c, 1 - y),
+    ):
+        signal(barrier, device)
+    signal_z(barrier)
 
     group = max(g for g in range(1, 33) if chunk % g == 0)
 
@@ -93,29 +141,114 @@
 
         @pl.loop(0, chunk // group)
         def _(i):
-            at = pl.multiple_of(i * (group * TILE), group * TILE)
-            v = gin[zt, :, pl.ds(at, group * TILE)].astype(jnp.float32)
+            first = pl.multiple_of(i * (group * TILE), group * TILE)
+            v = gin[zt, :, pl.ds(first, group * TILE)].astype(jnp.float32)
             packed[zt, pl.ds(i * group, group)] = v.reshape(group, 8, 128).astype(jnp.bfloat16)
 
-    def copy1(zt, src, dst):
+    def remote(src, dst, send, recv, device):
         return pltpu.make_async_remote_copy(
-            src_ref=packed.at[zt, pl.ds(dst * step, span)],
-            dst_ref=recv1.at[zt, src],
-            send_sem=send1,
-            recv_sem=got1.at[zt, src],
-            device_id=dev(z * plane + dst),
+            src_ref=src,
+            dst_ref=dst,
+            send_sem=send,
+            recv_sem=recv,
+            device_id=device,
             device_id_type=MESH,
         )
 
-    for k in range(1, n_out + 1):
-        zt = (z + k) % n_out
-        pack(zt)
-        if k == 1:
-            pl.semaphore_wait(barrier, n - 1)
-
-        @pl.loop(1, plane, unroll=True)
-        def _(q):
-            copy1(zt, p, (p + q) % plane).start()
+    def landed(ref, sem):
+        pltpu.make_async_copy(ref, ref, sem).wait()
+
+    def first_x(xx, cc):
+        return (xx * 2 + cc) * (2 * step) + span - hx
+
+    def first_y(xx, cc, yy):
+        return (xx * 4 + cc * 2 + yy) * step + yy * hx
+
+    def send_raw(zt):
+        for m in (3, 2, 1):
+            xx, cc = (1 - x if m >= 2 else x), (1 - c if m % 2 else c)
+            remote(
+                packed.at[zt, pl.ds(first_x(xx, cc), wx)],
+                r1x.at[zt, m - 1],
+                send1x,
+                got1x.at[zt],
+                at(z, xx, cc, y),
+            ).start()
+            yy = 1 - y if m >= 2 else y
+            for xb in range(2):
+                remote(
+                    packed.at[zt, pl.ds(first_y(xb, cc, yy), hy)],
+                    r1y.at[zt, m - 1, xb],
+                    send1y,
+                    got1y.at[zt],
+                    at(z, x, cc, yy),
+                ).start()
+
+    def sum_raw(zt):
+        landed(r1x.at[zt], got1x.at[zt])
+        own = first_x(x, c)
+
+        @pl.loop(0, wx, unroll=3)
+        def _(t):
+            acc = packed[zt, own + t].astype(jnp.float32) + r1x[zt, 0, t].astype(jnp.float32)
+            rest = r1x[zt, 1, t].astype(jnp.float32) + r1x[zt, 2, t].astype(jnp.float32)
+            sx[zt, t] = acc + rest
+
+        remote(
+            sx.at[zt, pl.ds((1 - y) * gap, hx)],
+            r2x.at[zt],
+            send2x,
+            got2x.at[zt],
+            at(z, x, c, 1 - y),
+        ).start()
+        landed(r1y.at[zt], got1y.at[zt])
+        for xb in range(2):
+            own = first_y(xb, c, y)
+
+            @pl.loop(0, hy, unroll=3)
+            def _(t):
+                acc = packed[zt, own + t].astype(jnp.float32)
+                acc = acc + r1y[zt, 0, xb, t].astype(jnp.float32)
+                rest = r1y[zt, 1, xb, t].astype(jnp.float32)
+                rest = rest + r1y[zt, 2, xb, t].astype(jnp.float32)
+                sy[zt, xb, t] = acc + rest
+
+        remote(
+            sy.at[zt, 1 - x],
+            r2y.at[zt],
+            send2y,
+            got2y.at[zt],
+            at(z, 1 - x, c, y),
+        ).start()
+
+    def copy3(zt, src):
+        return remote(part.at[zt], recv3.at[src], send3, got3, at(zt, x, c, y))
+
+    def sum_plane(zt):
+        landed(r2x.at[zt], got2x.at[zt])
+
+        @pl.loop(0, hx, unroll=2)
+        def _(t):
+            part[zt, (1 - y) * hy + t] = sx[zt, y * gap + t] + r2x[zt, t]
+
+        landed(r2y.at[zt], got2y.at[zt])
+
+        @pl.loop(0, hy, unroll=2)
+        def _(t):
+            part[zt, y * hx + t] = sy[zt, x, t] + r2y[zt, t]
+
+    pack(order[0])
+    pl.semaphore_wait(barrier, 5 + n_z)
+    send_raw(order[0])
+    signal_z(ready.at[0])
+    for k in range(1, n_out):
+        pack(order[k])
+        if k < AHEAD:
+            send_raw(order[k])
+    for i in range(n_out - 2):
+        pl.semaphore_wait(ready.at[i], n_z)
+        if i < n_out - 3:
+            signal_z(ready.at[i + 1])
 
     lane = lax.broadcasted_iota(jnp.int32, (rows, 128), 1)
     shift_l = off % 128
@@ -125,37 +258,28 @@
         mv_loads[j].wait()
         edge = jnp.pad(ref[pl.ds(whole, shard - whole)], (0, 128 - (shard - whole)))
         edge = jnp.broadcast_to(edge.reshape(1, 128), (8, 128))
-        x = jnp.concatenate([ref[pl.ds(0, whole)].reshape(step * 8, 128), edge], 0)
-        x = pltpu.roll(x, shift_l, 1)
-        x = jnp.where(lane < shift_l, pltpu.roll(x, 1, 0), x)
-        x = pltpu.roll(x, shift_r, 0)
-        mv[:, j] = x.reshape(span, 8, 128)
-    halo_copy = pltpu.make_async_remote_copy(
-        src_ref=mv.at[span - 1],
-        dst_ref=halo,
-        send_sem=halo_sem.at[0],
-        recv_sem=halo_sem.at[1],
-        device_id=dev((d + 1) % n),
-        device_id_type=MESH,
-    )
-    halo_copy.start()
+        w = jnp.concatenate([ref[pl.ds(0, whole)].reshape(step * 8, 128), edge], 0)
+        w = pltpu.roll(w, shift_l, 1)
+        w = jnp.where(lane < shift_l, pltpu.roll(w, 1, 0), w)
+        w = pltpu.roll(w, shift_r, 0)
+        mv[:, j] = w.reshape(span, 8, 128)
 
     place = lax.broadcasted_iota(jnp.int32, (8, 128), 0) * 128 + lax.broadcasted_iota(
         jnp.int32, (8, 128), 1
     )
     low = [offsets_ref[l] - base for l in range(layers)]
     high = [offsets_ref[l] + sizes_ref[l] - base for l in range(layers)]
-    own_low = [jnp.maximum(x, off) for x in low]
-    own_high = [jnp.minimum(x, off + shard) for x in high]
+    own_low = [jnp.maximum(v, off) for v in low]
+    own_high = [jnp.minimum(v, off + shard) for v in high]
     lane1 = lax.broadcasted_iota(jnp.int32, (1, 128), 1)
 
     def squares(value, first):
         def add(t, accs):
             pos = place + t * TILE
-            x = value(t)
-            x = x * x
+            v = value(t)
+            v = v * v
             return tuple(
-                acc + jnp.where((pos >= lo) & (pos < hi), x, 0.0)
+                acc + jnp.where((pos >= lo) & (pos < hi), v, 0.0)
                 for acc, lo, hi in zip(accs, own_low, own_high)
             )
 
@@ -169,68 +293,34 @@
 
     wrow[...] = squares(lambda t: mv[t, 0], 0)
 
-    def copy2(zt, src):
-        return pltpu.make_async_remote_copy(
-            src_ref=part.at[zt],
-            dst_ref=recv2.at[src],
-            send_sem=send2,
-            recv_sem=got2.at[src],
-            device_id=dev(zt * plane + p),
-            device_id_type=MESH,
-        )
-
-    for k in range(1, n_out + 1):
-        zt = (z + k) % n_out
-
-        @pl.loop(1, plane)
-        def _(q):
-            copy1(zt, (p + q) % plane, p).wait_recv()
-
-        @pl.loop(0, span)
-        def _(t):
-            acc = packed[zt, p * step + t].astype(jnp.float32)
-            for q in range(1, plane):
-                acc = acc + recv1[zt, (p + q) % plane, t].astype(jnp.float32)
-            part[zt, t] = acc
-
-        if k < n_out:
-            copy2(zt, z).start()
-
-    halo_copy.wait()
-    for j in range(2):
-        mv[0, j] = jnp.where(place < off, halo[j], mv[0, j])
-
-    @pl.loop(1, n_out)
-    def _(k):
-        copy2(z, (z + k) % n_out).wait_recv()
+    for k in range(n_out):
+        sum_raw(order[k])
+        if k + AHEAD < n_out:
+            send_raw(order[k + AHEAD])
+        if k > 0:
+            sum_plane(order[k - 1])
+            copy3(order[k - 1], z).start()
+    sum_plane(z)
+
+    landed(recv3.at[pl.ds(0, n_out - 1)], got3)
 
     @pl.loop(0, span)
     def _(t):
         acc = part[z, t]
         for k in range(1, n_out):
-            acc = acc + recv2[(z + k) % n_out, t]
+            acc = acc + recv3[(z + k) % n_out, t]
         grad_buf[t] = acc / n
 
     stats[d] = squares(lambda t: grad_buf[t], layers) + wrow[...]
-
-    def copy3(src, dst):
-        return pltpu.make_async_remote_copy(
-            src_ref=stats.at[src],
-            dst_ref=stats.at[src],
-            send_sem=send3,
-            recv_sem=got3.at[src],
-            device_id=dev(dst),
-            device_id_type=MESH,
-        )
 
     @pl.loop(1, n, unroll=True)
     def _(q):
-        copy3(d, (d + q) % n).start()
-
-    @pl.loop(1, n, unroll=True)
-    def _(q):
-        copy3((d + q) % n, d).wait_recv()
-
+        remote(stats.at[d], stats.at[d], send_s, got_s, dev((d + q) % n)).start()
+
+    halo_copy = remote(mv.at[span - 1], halo, halo_sem.at[0], halo_sem.at[1], dev((d + 1) % n))
+    halo_copy.start()
+
+    landed(stats.at[pl.ds(0, n - 1)], got_s)
     total = jnp.sum(stats[...], axis=0)
     trust, decay = [], []
     for l in range(layers):
@@ -242,6 +332,10 @@
         ratio = 0.02 * wnorm / (gnorm + 0.001 * wnorm + 1e-06)
         trust.append(skipped + (1.0 - skipped) * ratio)
         decay.append((1.0 - skipped) * 0.001)
+
+    halo_copy.wait()
+    for j in range(2):
+        mv[0, j] = jnp.where(place < off, halo[j], mv[0, j])
 
     @pl.loop(0, span)
     def _(t):
@@ -259,77 +353,67 @@
         nmw[t] = nm
         ags[d, t] = nm.astype(jnp.bfloat16)
 
-    def copy4(block, dst):
-        return pltpu.make_async_remote_copy(
-            src_ref=ags.at[block],
-            dst_ref=ags.at[block],
-            send_sem=send4,
-            recv_sem=got4.at[block],
-            device_id=dev(dst),
-            device_id_type=MESH,
-        )
-
-    n_same = plane // 2
-    me_same = a * n_spa + s
-    partner = z * plane + a * (2 * n_spa) + (1 - c) * n_spa + s
-
-    def same(index, core):
-        return (index // n_spa) * (2 * n_spa) + core * n_spa + index % n_spa
-
-    def to_plane(zz):
-        block = zz * plane + p
-
-        @pl.loop(1, n_same)
-        def _(q):
-            peer = (me_same + q) % n_same
-            copy4(block, z * plane + same(peer, c)).start()
-
-    def to_partner(zz, index):
-        block = zz * plane + same(index, c)
-        copy4(block, partner).start()
-
-    @pl.loop(1, n_out)
-    def _(k):
-        zz = (z + k) % n_out
-        copy4(d, zz * plane + p).start()
-
-    to_plane(z)
-    to_partner(z, me_same)
-
-    @pl.loop(1, n_out)
-    def _(k):
-        zz = (z + k) % n_out
-        copy4(zz * plane + p, d).wait_recv()
-        to_plane(zz)
-        to_partner(zz, me_same)
+    def block(zz, xx, cc, yy):
+        return zz * plane + xx * 4 + cc * 2 + yy
+
+    def forward(b, device, lo=0, size=span):
+        piece = ags.at[b, pl.ds(lo, size)]
+        remote(piece, piece, send4, got4.at[b], device).start()
+
+    def arrived(b):
+        landed(ags.at[b], got4.at[b])
+
+    x_side = at(z, 1 - x, c, y)
+    y_side = at(z, x, c, 1 - y)
+    partner = at(z, x, 1 - c, y)
+    for k in range(1, n_out):
+        forward(d, at(flip(z, k), x, c, y))
+
+    def column(k):
+        b = block(flip(z, k), x, c, y)
+        if k > 0:
+            arrived(b)
+        forward(b, x_side)
+        forward(b, y_side)
+        forward(b, partner)
+
+    column(0)
+    for k in range(n_out):
+        zz = flip(z, k)
+        if k + 1 < n_out:
+            column(k + 1)
+        b = block(zz, x, c, 1 - y)
+        arrived(b)
+        forward(b, x_side, 0, hx)
+        forward(b, partner)
+        b = block(zz, 1 - x, c, y)
+        arrived(b)
+        forward(b, y_side, hx, hy)
+        forward(b, partner)
+        if k > 0:
+            b = block(flip(z, k - 1), 1 - x, c, 1 - y)
+            arrived(b)
+            forward(b, partner)
+    b = block(flip(z, n_out - 1), 1 - x, c, 1 - y)
+    arrived(b)
+    forward(b, partner)
 
     @pl.loop(0, n_out)
     def _(k):
-        zz = (z + k) % n_out
-
-        @pl.loop(1, n_same)
-        def _(q):
-            peer = (me_same + q) % n_same
-            copy4(zz * plane + same(peer, c), d).wait_recv()
-            to_partner(zz, peer)
-
-    @pl.loop(0, n_out)
-    def _(k):
-        zz = (z + k) % n_out
-
-        @pl.loop(0, n_same)
-        def _(q):
-            peer = (me_same + q) % n_same
-            block = zz * plane + same(peer, 1 - c)
-            copy4(block, d).wait_recv()
+        for xx in range(2):
+            for yy in range(2):
+                arrived(block(k, xx, 1 - c, yy))
 
     for ref, sem in (
-        (recv1.at[:, pl.ds(0, plane - 1)], send1),
-        (recv2.at[pl.ds(0, n_out - 1)], send2),
-        (stats.at[pl.ds(0, n - 1)], send3),
+        (r1x, send1x),
+        (r1y, send1y),
+        (r2x, send2x),
+        (r2y, send2y),
+        (recv3.at[pl.ds(0, n_out - 1)], send3),
+        (stats.at[pl.ds(0, n - 1)], send_s),
         (ags.at[pl.ds(0, n - 1)], send4),
     ):
-        pltpu.make_async_copy(ref, ref, sem).wait()
+        landed(ref, sem)
 
 
 def finish(plan, ags, nmw, nvw, out_ref, nm_ref, nv_ref, nm_out, nv_out, out_sem, own_sem):
@@ -375,15 +459,17 @@
     shard = master.shape[0]
     params = grads.shape[2]
     layers = layer_offsets.shape[0]
-    n_in = math.isqrt(n_rep)
-    n_out, n_a = n_rep // n_in, n_in // 2
+    plane = 8
     n = n_rep * n_spa
-    plane = n_in * n_spa
+    n_out = n // plane
     step = shard // TILE
     span = params // TILE - (n - 1) * step
     chunk = (plane - 1) * step + span
     tiles = params // TILE
-    plan = (n_out, n_a, n_spa, shard, step, span, layers)
+    hx = (span + 1) // 2
+    hy = span - hx
+    wx = step + 2 * hx - span
+    plan = (n_out, shard, step, span, layers)
     vmem = pl.BlockSpec(memory_space=pltpu.VMEM)
     smem = pl.BlockSpec(memory_space=pltpu.SMEM)
     anywhere = pl.BlockSpec(memory_space=pltpu.HBM)
@@ -403,7 +489,12 @@
             pltpu.VMEM((shard,), f32),
             pltpu.VMEM((n_out, 1, chunk * TILE), bf16),
             pltpu.VMEM((n_out, chunk, 8, 128), bf16),
-            pltpu.VMEM((n_out, plane, span, 8, 128), bf16),
+            pltpu.VMEM((n_out, 3, wx, 8, 128), bf16),
+            pltpu.VMEM((n_out, 3, 2, hy, 8, 128), bf16),
+            pltpu.VMEM((n_out, wx, 8, 128), f32),
+            pltpu.VMEM((n_out, 2, hy, 8, 128), f32),
+            pltpu.VMEM((n_out, hx, 8, 128), f32),
+            pltpu.VMEM((n_out, hy, 8, 128), f32),
             pltpu.VMEM((n_out, span, 8, 128), f32),
             pltpu.VMEM((n_out, span, 8, 128), f32),
             pltpu.VMEM((span, 2, 8, 128), f32),
@@ -413,13 +504,20 @@
             pltpu.VMEM((n, 1, 128), f32),
             dma((n_out,)),
             dma((2,)),
-            dma(()),
-            dma((n_out, plane)),
+            pltpu.SemaphoreType.REGULAR((n_out,)),
             dma(()),
             dma((n_out,)),
+            dma(()),
+            dma((n_out,)),
+            dma(()),
+            dma((n_out,)),
+            dma(()),
+            dma((n_out,)),
+            dma(()),
+            dma(()),
             dma((2,)),
             dma(()),
-            dma((n,)),
+            dma(()),
             dma(()),
             dma((n,)),
         ],
@@ -450,11 +548,13 @@
 def tiled(n_rep, n_spa, params):
     n = n_rep * n_spa
     shard = params // n
-    n_in = math.isqrt(n_rep)
     rest = shard % TILE
+    n_out = n_rep // 4
     return (
-        n_in * n_in == n_rep
-        and n_in % 2 == 0
+        n_spa == 2
+        and n_rep % 4 == 0
+        and n_out >= 2
+        and n_out & (n_out - 1) == 0
         and params % TILE == 0
         and shard >= TILE
         and 0 < n * rest <= TILE

time: 53 us -> 48.5 us (0.915)
  Pallas kernels: 52.2 us -> 47.7 us
    pallas_call x1, Pallas kernels: 50.6 us -> 46.1 us  [windowed(): pl.pallas_call(functools.partial(kernel, plan), out_shape=(pltpu.VMEM((n,...]
where the time goes in v1:
time: 48.5 us; the launch traced here: 48.3 us
  Pallas kernels  47.7 us (98%)
  between operations  0.64 us (1%)
    pallas_call x1, Pallas kernels, windowed(): pl.pallas_call(functools.partial(kernel, plan), out_shape=(pltpu.VMEM((n,...  46.1 us
    pallas_call x1, Pallas kernels, windowed(): pl.pallas_call(functools.partial(finish, (n, n_spa, shard, step, span)),...  1.57 us

profile of v1, /device:TPU:0, one launch (start us, length us, event | category | flops | bytes accessed | tf_op | source)
XLA Modules:
  0.0 48.3 jit_solution(373422829234210608)
XLA Ops:
  0.6 46.1 %shard_map.85 = (bf16[32,27,8,128]{3,2,1,0:T(8,128)(2,1)S(1)}, f32[27,8,128]{2,1,0:T(8,128)S(1)}, f32[27,8,128]{2,1,0:T(8,128)S(1)}) custom-call(bf16[1,1,852992]{2,1,0:T(2,128)(2,1)} %grads_ref.1, f32[26656]{0:T(1024)} %m_ref.1, f32[26656]{0:T(1024)} %v_ref.1, s32[6]{0:T(128)} %offsets_ref.1, s32[6]{0:T(128)} %sizes_ref.1, s32[6]{0:T(128)} %skip_ref.1), custom_call_target="tpu_custom_call" | custom-call | tf_op jit(solution)/shard_map/pallas_call | solution.py:478
  46.8 1.6 %shard_map.86 = (bf16[833,8,128]{2,1,0:T(8,128)(2,1)}, f32[26656]{0:T(1024)}, f32[26656]{0:T(1024)}) custom-call(bf16[32,27,8,128]{3,2,1,0:T(8,128)(2,1)S(1)} %get-tuple-element.9.ags, f32[27,8,128]{2,1,0:T(8,128)S(1)} %get-tuple-element.10.nmw, f32[27,8,128]{2,1,0:T(8,128)S(1)} %get-tuple-element.11.nvw), custom_call_target="tpu_custom_call" | custom-call | tf_op jit(solution)/shard_map/pallas_call | solution.py:528

commit v2 on v1

--- a/solution.py
+++ b/solution.py
@@ -9,7 +9,11 @@
 
 MESH = pl.DeviceIdType.MESH
 TILE = 1024
-AHEAD = 2
+ZTILES = 4
+RS = "k1 bar A1 B1 k2 A2 k3 k4 z1 z2 z3 mv s1 B2 A3 s2 p1 B3 A4 s3 p2 B4 Z s4 p3 p4"
+ZSEND = (1, 2, 3)
+ZWAIT = (1, 2, 3)
+DIRECT = (0, 3)
 
 
 def flip(i, k):
@@ -42,6 +46,9 @@
     sy,
     r2x,
     r2y,
+    rz1,
+    zs,
+    rz2,
     part,
     recv3,
     mv,
@@ -60,6 +67,10 @@
     got2x,
     send2y,
     got2y,
+    sendz1,
+    gotz1,
+    sendz2,
+    gotz2,
     send3,
     got3,
     halo_sem,
@@ -68,15 +79,14 @@
     send4,
     got4,
 ):
-    n_out, shard, step, span, layers = plan
+    n_out, shard, step, span, layers, hx, hy, hz = plan
     plane = 8
     n = n_out * plane
     chunk = (plane - 1) * step + span
     rows = span * 8
-    hx = (span + 1) // 2
-    hy = span - hx
-    wx = step + 2 * hx - span
-    gap = wx - hx
+    hxy = hx + hy
+    half_a = (span + 1) // 2
+    half_b = span - half_a
     r = lax.axis_index("replica")
     y = lax.axis_index("spatial")
     d = r * 2 + y
@@ -114,14 +124,16 @@
     def signal(sem, device):
         pl.semaphore_signal(sem, inc=1, device_id=device, device_id_type=MESH)
 
-    def signal_z(sem):
+    def signal_z(sem, cores):
         @pl.when(z > 0)
         def _():
-            signal(sem, at(z - 1, x, c, y))
+            for cc in cores:
+                signal(sem, at(z - 1, x, cc, y))
 
         @pl.when(z < n_out - 1)
         def _():
-            signal(sem, at(z + 1, x, c, y))
+            for cc in cores:
+                signal(sem, at(z + 1, x, cc, y))
 
     n_z = jnp.where(z > 0, 1, 0) + jnp.where(z < n_out - 1, 1, 0)
     for device in (
@@ -132,7 +144,7 @@
         at(z, x, 1 - c, 1 - y),
     ):
         signal(barrier, device)
-    signal_z(barrier)
+    signal_z(barrier, (c, 1 - c))
 
     group = max(g for g in range(1, 33) if chunk % g == 0)
 
@@ -158,103 +170,117 @@
     def landed(ref, sem):
         pltpu.make_async_copy(ref, ref, sem).wait()
 
-    def first_x(xx, cc):
-        return (xx * 2 + cc) * (2 * step) + span - hx
-
-    def first_y(xx, cc, yy):
-        return (xx * 4 + cc * 2 + yy) * step + yy * hx
-
-    def send_raw(zt):
+    def first(xx, cc, yy):
+        return (xx * 4 + cc * 2 + yy) * step
+
+    def send_raw(zt, h):
+        yb, xb = (y, x) if h else (1 - y, 1 - x)
         for m in (3, 2, 1):
             xx, cc = (1 - x if m >= 2 else x), (1 - c if m % 2 else c)
             remote(
-                packed.at[zt, pl.ds(first_x(xx, cc), wx)],
-                r1x.at[zt, m - 1],
+                packed.at[zt, pl.ds(first(xx, cc, yb), hx)],
+                r1x.at[h, zt, m - 1],
                 send1x,
-                got1x.at[zt],
+                got1x.at[h, zt],
                 at(z, xx, cc, y),
             ).start()
             yy = 1 - y if m >= 2 else y
-            for xb in range(2):
-                remote(
-                    packed.at[zt, pl.ds(first_y(xb, cc, yy), hy)],
-                    r1y.at[zt, m - 1, xb],
-                    send1y,
-                    got1y.at[zt],
-                    at(z, x, cc, yy),
-                ).start()
+            remote(
+                packed.at[zt, pl.ds(first(xb, cc, yy) + hx, hy)],
+                r1y.at[h, zt, m - 1],
+                send1y,
+                got1y.at[h, zt],
+                at(z, x, cc, yy),
+            ).start()
+
+    def raws(zt, h, t, r1, own):
+        v = packed[zt, own + t].astype(jnp.float32) + r1[h, zt, 0, t].astype(jnp.float32)
+        return v + (r1[h, zt, 1, t].astype(jnp.float32) + r1[h, zt, 2, t].astype(jnp.float32))
 
     def sum_raw(zt):
-        landed(r1x.at[zt], got1x.at[zt])
-        own = first_x(x, c)
-
-        @pl.loop(0, wx, unroll=3)
+        landed(r1x.at[0, zt], got1x.at[0, zt])
+        own = first(x, c, 1 - y)
+
+        @pl.loop(0, hx, unroll=2)
         def _(t):
-            acc = packed[zt, own + t].astype(jnp.float32) + r1x[zt, 0, t].astype(jnp.float32)
-            rest = r1x[zt, 1, t].astype(jnp.float32) + r1x[zt, 2, t].astype(jnp.float32)
-            sx[zt, t] = acc + rest
-
-        remote(
-            sx.at[zt, pl.ds((1 - y) * gap, hx)],
-            r2x.at[zt],
-            send2x,
-            got2x.at[zt],
-            at(z, x, c, 1 - y),
-        ).start()
-        landed(r1y.at[zt], got1y.at[zt])
-        for xb in range(2):
-            own = first_y(xb, c, y)
-
-            @pl.loop(0, hy, unroll=3)
-            def _(t):
-                acc = packed[zt, own + t].astype(jnp.float32)
-                acc = acc + r1y[zt, 0, xb, t].astype(jnp.float32)
-                rest = r1y[zt, 1, xb, t].astype(jnp.float32)
-                rest = rest + r1y[zt, 2, xb, t].astype(jnp.float32)
-                sy[zt, xb, t] = acc + rest
-
-        remote(
-            sy.at[zt, 1 - x],
-            r2y.at[zt],
-            send2y,
-            got2y.at[zt],
-            at(z, 1 - x, c, y),
-        ).start()
+            sx[zt, t] = raws(zt, 0, t, r1x, own)
+
+        remote(sx.at[zt], r2x.at[zt], send2x, got2x.at[zt], at(z, x, c, 1 - y)).start()
+        landed(r1y.at[0, zt], got1y.at[0, zt])
+        own2 = first(1 - x, c, y) + hx
+
+        @pl.loop(0, hy, unroll=2)
+        def _(t):
+            sy[zt, t] = raws(zt, 0, t, r1y, own2)
+
+        remote(sy.at[zt], r2y.at[zt], send2y, got2y.at[zt], at(z, 1 - x, c, y)).start()
 
     def copy3(zt, src):
         return remote(part.at[zt], recv3.at[src], send3, got3, at(zt, x, c, y))
 
     def sum_plane(zt):
+        own = first(x, c, y)
+        landed(r1x.at[1, zt], got1x.at[1, zt])
         landed(r2x.at[zt], got2x.at[zt])
 
         @pl.loop(0, hx, unroll=2)
         def _(t):
-            part[zt, (1 - y) * hy + t] = sx[zt, y * gap + t] + r2x[zt, t]
-
+            part[zt, t] = raws(zt, 1, t, r1x, own) + r2x[zt, t]
+
+        landed(r1y.at[1, zt], got1y.at[1, zt])
         landed(r2y.at[zt], got2y.at[zt])
 
         @pl.loop(0, hy, unroll=2)
         def _(t):
-            part[zt, y * hx + t] = sy[zt, x, t] + r2y[zt, t]
-
-    pack(order[0])
-    pl.semaphore_wait(barrier, 5 + n_z)
-    send_raw(order[0])
-    signal_z(ready.at[0])
-    for k in range(1, n_out):
-        pack(order[k])
-        if k < AHEAD:
-            send_raw(order[k])
-    for i in range(n_out - 2):
-        pl.semaphore_wait(ready.at[i], n_z)
-        if i < n_out - 3:
-            signal_z(ready.at[i + 1])
+            part[zt, hx + t] = raws(zt, 1, t, r1y, own + hx) + r2y[zt, t]
+
+    def send_far(zt, other):
+        cc = 1 - c if other else c
+        for j in range(4):
+            remote(
+                packed.at[zt, pl.ds(first(j // 2, cc, j % 2) + hxy, hz)],
+                rz1.at[other * n_out + z, j],
+                sendz1,
+                gotz1,
+                at(zt, x, cc, y),
+            ).start()
+
+    def send_distance(j):
+        @pl.when(z >= j)
+        def _():
+            for other in (0, 1):
+                send_far(z - j, other)
+
+        @pl.when(z < n_out - j)
+        def _():
+            for other in (0, 1):
+                send_far(z + j, other)
+
+    def sum_far():
+        landed(rz1.at[pl.ds(0, 2 * n_out - 1)], gotz1)
+
+        @pl.loop(0, 4)
+        def _(j):
+            own = first(j // 2, c, j % 2) + hxy
+            for t in range(hz):
+                acc = packed[z, own + t].astype(jnp.float32)
+                acc = acc + rz1[n_out + z, j, t].astype(jnp.float32)
+                for k in range(1, n_out):
+                    zz = (z + k) % n_out
+                    two = rz1[zz, j, t].astype(jnp.float32)
+                    acc = acc + (two + rz1[n_out + zz, j, t].astype(jnp.float32))
+                zs[j, t] = acc
+
+        for m in (3, 2, 1):
+            xx, yy = (1 - x if m >= 2 else x), (1 - y if m % 2 else y)
+            remote(zs.at[xx * 2 + yy], rz2.at[m - 1], sendz2, gotz2, at(z, xx, c, yy)).start()
 
     lane = lax.broadcasted_iota(jnp.int32, (rows, 128), 1)
     shift_l = off % 128
     shift_r = off // 128
     whole = step * TILE
-    for j, ref in enumerate((m_in, v_in)):
+
+    def window(j, ref):
         mv_loads[j].wait()
         edge = jnp.pad(ref[pl.ds(whole, shard - whole)], (0, 128 - (shard - whole)))
         edge = jnp.broadcast_to(edge.reshape(1, 128), (8, 128))
@@ -291,25 +317,56 @@
             row = jnp.where(lane1 == first + l, jnp.sum(acc, axis=(0, 1), keepdims=True), row)
         return row
 
-    wrow[...] = squares(lambda t: mv[t, 0], 0)
-
-    for k in range(n_out):
-        sum_raw(order[k])
-        if k + AHEAD < n_out:
-            send_raw(order[k + AHEAD])
-        if k > 0:
-            sum_plane(order[k - 1])
-            copy3(order[k - 1], z).start()
-    sum_plane(z)
+    def step_z(j):
+        if j == 1:
+            send_distance(1)
+            send_far(z, 1)
+            return
+        pl.semaphore_wait(ready.at[j - 2], n_z)
+        if j < n_out - 1:
+            signal_z(ready.at[j - 1], (c,))
+        send_distance(j)
+
+    for op in RS.split():
+        i = int(op[1:] or 0) if op != "bar" and op != "mv" else 0
+        zt = order[i - 1]
+        if op == "bar":
+            pl.semaphore_wait(barrier, 5 + 2 * n_z)
+            signal_z(ready.at[0], (c,))
+        elif op == "mv":
+            for j, ref in enumerate((m_in, v_in)):
+                window(j, ref)
+            wrow[...] = squares(lambda t: mv[t, 0], 0)
+        elif op[0] == "k":
+            pack(zt)
+        elif op[0] == "A":
+            send_raw(zt, 0)
+        elif op[0] == "B":
+            send_raw(zt, 1)
+        elif op[0] == "z":
+            step_z(i)
+        elif op[0] == "Z":
+            sum_far()
+        elif op[0] == "s":
+            sum_raw(zt)
+        elif op[0] == "p":
+            sum_plane(zt)
+            if i < n_out:
+                copy3(zt, z).start()
 
     landed(recv3.at[pl.ds(0, n_out - 1)], got3)
 
-    @pl.loop(0, span)
+    @pl.loop(0, hxy)
     def _(t):
         acc = part[z, t]
         for k in range(1, n_out):
             acc = acc + recv3[(z + k) % n_out, t]
         grad_buf[t] = acc / n
+
+    landed(rz2, gotz2)
+    for t in range(hz):
+        acc = zs[x * 2 + y, t] + rz2[0, t]
+        grad_buf[hxy + t] = (acc + (rz2[1, t] + rz2[2, t])) / n
 
     stats[d] = squares(lambda t: grad_buf[t], layers) + wrow[...]
 
@@ -365,8 +422,9 @@
 
     x_side = at(z, 1 - x, c, y)
     y_side = at(z, x, c, 1 - y)
+    across = at(z, 1 - x, c, 1 - y)
     partner = at(z, x, 1 - c, y)
-    for k in range(1, n_out):
+    for k in ZSEND:
         forward(d, at(flip(z, k), x, c, y))
 
     def column(k):
@@ -375,28 +433,37 @@
             arrived(b)
         forward(b, x_side)
         forward(b, y_side)
+        if k in DIRECT:
+            forward(b, across)
         forward(b, partner)
 
-    column(0)
-    for k in range(n_out):
+    def sides(k):
         zz = flip(z, k)
-        if k + 1 < n_out:
-            column(k + 1)
         b = block(zz, x, c, 1 - y)
         arrived(b)
-        forward(b, x_side, 0, hx)
+        if k not in DIRECT:
+            forward(b, x_side, 0, half_a)
         forward(b, partner)
         b = block(zz, 1 - x, c, y)
         arrived(b)
-        forward(b, y_side, hx, hy)
+        if k not in DIRECT:
+            forward(b, y_side, half_a, half_b)
         forward(b, partner)
-        if k > 0:
-            b = block(flip(z, k - 1), 1 - x, c, 1 - y)
-            arrived(b)
-            forward(b, partner)
-    b = block(flip(z, n_out - 1), 1 - x, c, 1 - y)
-    arrived(b)
-    forward(b, partner)
+
+    def corner(k):
+        b = block(flip(z, k), 1 - x, c, 1 - y)
+        arrived(b)
+        forward(b, partner)
+
+    visits = (0,) + ZWAIT
+    column(0)
+    for i, k in enumerate(visits):
+        if i + 1 < n_out:
+            column(visits[i + 1])
+        sides(k)
+        if i > 0:
+            corner(visits[i - 1])
+    corner(visits[-1])
 
     @pl.loop(0, n_out)
     def _(k):
@@ -409,6 +476,8 @@
         (r1y, send1y),
         (r2x, send2x),
         (r2y, send2y),
+        (rz1.at[pl.ds(0, 2 * n_out - 1)], sendz1),
+        (rz2, sendz2),
         (recv3.at[pl.ds(0, n_out - 1)], send3),
         (stats.at[pl.ds(0, n - 1)], send_s),
         (ags.at[pl.ds(0, n - 1)], send4),
@@ -466,10 +535,10 @@
     span = params // TILE - (n - 1) * step
     chunk = (plane - 1) * step + span
     tiles = params // TILE
-    hx = (span + 1) // 2
-    hy = span - hx
-    wx = step + 2 * hx - span
-    plan = (n_out, shard, step, span, layers)
+    hz = ZTILES
+    hx = (span - hz + 1) // 2
+    hy = span - hz - hx
+    plan = (n_out, shard, step, span, layers, hx, hy, hz)
     vmem = pl.BlockSpec(memory_space=pltpu.VMEM)
     smem = pl.BlockSpec(memory_space=pltpu.SMEM)
     anywhere = pl.BlockSpec(memory_space=pltpu.HBM)
@@ -489,14 +558,17 @@
             pltpu.VMEM((shard,), f32),
             pltpu.VMEM((n_out, 1, chunk * TILE), bf16),
             pltpu.VMEM((n_out, chunk, 8, 128), bf16),
-            pltpu.VMEM((n_out, 3, wx, 8, 128), bf16),
-            pltpu.VMEM((n_out, 3, 2, hy, 8, 128), bf16),
-            pltpu.VMEM((n_out, wx, 8, 128), f32),
-            pltpu.VMEM((n_out, 2, hy, 8, 128), f32),
+            pltpu.VMEM((2, n_out, 3, hx, 8, 128), bf16),
+            pltpu.VMEM((2, n_out, 3, hy, 8, 128), bf16),
             pltpu.VMEM((n_out, hx, 8, 128), f32),
             pltpu.VMEM((n_out, hy, 8, 128), f32),
-            pltpu.VMEM((n_out, span, 8, 128), f32),
-            pltpu.VMEM((n_out, span, 8, 128), f32),
+            pltpu.VMEM((n_out, hx, 8, 128), f32),
+            pltpu.VMEM((n_out, hy, 8, 128), f32),
+            pltpu.VMEM((2 * n_out, 4, hz, 8, 128), bf16),
+            pltpu.VMEM((4, hz, 8, 128), f32),
+            pltpu.VMEM((3, hz, 8, 128), f32),
+            pltpu.VMEM((n_out, hx + hy, 8, 128), f32),
+            pltpu.VMEM((n_out, hx + hy, 8, 128), f32),
             pltpu.VMEM((span, 2, 8, 128), f32),
             pltpu.VMEM((2, 8, 128), f32),
             pltpu.VMEM((span, 8, 128), f32),
@@ -506,13 +578,17 @@
             dma((2,)),
             pltpu.SemaphoreType.REGULAR((n_out,)),
             dma(()),
+            dma((2, n_out)),
+            dma(()),
+            dma((2, n_out)),
+            dma(()),
             dma((n_out,)),
             dma(()),
             dma((n_out,)),
             dma(()),
-            dma((n_out,)),
-            dma(()),
-            dma((n_out,)),
+            dma(()),
+            dma(()),
+            dma(()),
             dma(()),
             dma(()),
             dma((2,)),

time: 48.5 us -> 44.3 us (0.913)
  Pallas kernels: 47.7 us -> 43.5 us
    pallas_call x1, Pallas kernels: 46.1 us -> 41.9 us  [windowed(): pl.pallas_call(functools.partial(kernel, plan), out_shape=(pltpu.VMEM((n,...]
where the time goes in v2:
time: 44.3 us; the launch traced here: 44.1 us
  Pallas kernels  43.5 us (98%)
  between operations  0.64 us (1%)
    pallas_call x1, Pallas kernels, windowed(): pl.pallas_call(functools.partial(kernel, plan), out_shape=(pltpu.VMEM((n,...  41.9 us
    pallas_call x1, Pallas kernels, windowed(): pl.pallas_call(functools.partial(finish, (n, n_spa, shard, step, span)),...  1.57 us

profile of v2, /device:TPU:0, one launch (start us, length us, event | category | flops | bytes accessed | tf_op | source)
XLA Modules:
  0.0 44.1 jit_solution(11063551082034171601)
XLA Ops:
  0.6 41.9 %shard_map.85 = (bf16[32,27,8,128]{3,2,1,0:T(8,128)(2,1)S(1)}, f32[27,8,128]{2,1,0:T(8,128)S(1)}, f32[27,8,128]{2,1,0:T(8,128)S(1)}) custom-call(bf16[1,1,852992]{2,1,0:T(2,128)(2,1)} %grads_ref.1, f32[26656]{0:T(1024)} %m_ref.1, f32[26656]{0:T(1024)} %v_ref.1, s32[6]{0:T(128)} %offsets_ref.1, s32[6]{0:T(128)} %sizes_ref.1, s32[6]{0:T(128)} %skip_ref.1), custom_call_target="tpu_custom_call" | custom-call | tf_op jit(solution)/shard_map/pallas_call | solution.py:547
  42.5 1.6 %shard_map.86 = (bf16[833,8,128]{2,1,0:T(8,128)(2,1)}, f32[26656]{0:T(1024)}, f32[26656]{0:T(1024)}) custom-call(bf16[32,27,8,128]{3,2,1,0:T(8,128)(2,1)S(1)} %get-tuple-element.9.ags, f32[27,8,128]{2,1,0:T(8,128)S(1)} %get-tuple-element.10.nmw, f32[27,8,128]{2,1,0:T(8,128)S(1)} %get-tuple-element.11.nvw), custom_call_target="tpu_custom_call" | custom-call | tf_op jit(solution)/shard_map/pallas_call | solution.py:604

commit v3 on v2

--- a/solution.py
+++ b/solution.py
@@ -9,10 +9,17 @@
 
 MESH = pl.DeviceIdType.MESH
 TILE = 1024
-ZTILES = 4
-RS = "k1 bar A1 B1 k2 A2 k3 k4 z1 z2 z3 mv s1 B2 A3 s2 p1 B3 A4 s3 p2 B4 Z s4 p3 p4"
+ZTILES = 5
+XOR = (2, 3, 1, 0)
+RS = (
+    "k1", "bar", "A1", "B1", "k2", "A2", "k3", "k4", "z1", "z2", "z3", "mv", "s1", "B2", "A3",
+    "s2", "p1", "B3", "A4", "s3", "p2", "B4", "Z", "s4", "p3", "p4",
+)
 ZSEND = (1, 2, 3)
-ZWAIT = (1, 2, 3)
+AG = (
+    "c0", "c1", "g0", "x0", "y0", "c2", "e0", "c3", "x1", "y1", "d0", "x2", "y2", "d1", "h1",
+    "h2", "h3", "x3", "y3", "d2", "d3",
+)
 DIRECT = (0, 3)
 
 
@@ -30,12 +37,17 @@
     grads_ref,
     m_ref,
     v_ref,
+    offsets_in,
+    sizes_in,
+    skip_in,
+    ags,
+    agz,
+    age,
+    nmw,
+    nvw,
     offsets_ref,
     sizes_ref,
     skip_ref,
-    ags,
-    nmw,
-    nvw,
     m_in,
     v_in,
     gin,
@@ -49,6 +61,9 @@
     rz1,
     zs,
     rz2,
+    re1,
+    ze,
+    re2,
     part,
     recv3,
     mv,
@@ -58,6 +73,7 @@
     stats,
     in_sem,
     mv_sem,
+    table_sem,
     ready,
     send1x,
     got1x,
@@ -71,6 +87,10 @@
     gotz1,
     sendz2,
     gotz2,
+    send_e1,
+    got_e1,
+    send_e2,
+    got_e2,
     send3,
     got3,
     halo_sem,
@@ -78,6 +98,13 @@
     got_s,
     send4,
     got4,
+    send_g,
+    got_in,
+    got_gz,
+    got_gc,
+    send_e,
+    got_e,
+    back_sem,
 ):
     n_out, shard, step, span, layers, hx, hy, hz = plan
     plane = 8
@@ -85,8 +112,9 @@
     chunk = (plane - 1) * step + span
     rows = span * 8
     hxy = hx + hy
-    half_a = (span + 1) // 2
-    half_b = span - half_a
+    last = n_out - 1
+    half_a = (hxy + 1) // 2
+    half_b = hxy - half_a
     r = lax.axis_index("replica")
     y = lax.axis_index("spatial")
     d = r * 2 + y
@@ -112,13 +140,21 @@
         )
 
     order = [(z + k) % n_out for k in range(1, n_out + 1)]
+    if XOR:
+        order = [flip(z, k) for k in XOR]
     for zt in order:
         load(zt).start()
     mv_loads = [
         pltpu.make_async_copy(ref, buf, mv_sem.at[j])
         for j, (ref, buf) in enumerate(((m_ref, m_in), (v_ref, v_in)))
     ]
-    for copy in mv_loads:
+    tables = [
+        pltpu.make_async_copy(ref, buf, table_sem.at[j])
+        for j, (ref, buf) in enumerate(
+            ((offsets_in, offsets_ref), (sizes_in, sizes_ref), (skip_in, skip_ref))
+        )
+    ]
+    for copy in mv_loads + tables:
         copy.start()
 
     def signal(sem, device):
@@ -148,9 +184,9 @@
 
     group = max(g for g in range(1, 33) if chunk % g == 0)
 
-    def pack(zt):
+    def pack(k):
+        zt = order[k - 1]
         load(zt).wait()
-
         @pl.loop(0, chunk // group)
         def _(i):
             first = pl.multiple_of(i * (group * TILE), group * TILE)
@@ -245,6 +281,16 @@
                 at(zt, x, cc, y),
             ).start()
 
+        @pl.when((zt == last) & (cc == 1))
+        def _():
+            remote(
+                packed.at[last, pl.ds(chunk - 1, 1)],
+                re1.at[pl.ds(z * 2 + c, 1)],
+                send_e1,
+                got_e1,
+                at(zt, x, cc, y),
+            ).start()
+
     def send_distance(j):
         @pl.when(z >= j)
         def _():
@@ -275,6 +321,20 @@
             xx, yy = (1 - x if m >= 2 else x), (1 - y if m % 2 else y)
             remote(zs.at[xx * 2 + yy], rz2.at[m - 1], sendz2, gotz2, at(z, xx, c, yy)).start()
 
+        @pl.when((z == last) & (c == 1))
+        def _():
+            landed(re1.at[pl.ds(0, 2 * n_out - 1)], got_e1)
+            acc = packed[last, chunk - 1].astype(jnp.float32)
+            for j in range(2 * n_out - 1):
+                acc = acc + re1[j].astype(jnp.float32)
+            ze[0] = acc
+
+            @pl.when(x * 2 + y < 3)
+            def _():
+                remote(
+                    ze, re2.at[pl.ds(x * 2 + y, 1)], send_e2, got_e2, at(z, 1, 1, 1)
+                ).start()
+
     lane = lax.broadcasted_iota(jnp.int32, (rows, 128), 1)
     shift_l = off % 128
     shift_r = off // 128
@@ -293,20 +353,27 @@
     place = lax.broadcasted_iota(jnp.int32, (8, 128), 0) * 128 + lax.broadcasted_iota(
         jnp.int32, (8, 128), 1
     )
-    low = [offsets_ref[l] - base for l in range(layers)]
-    high = [offsets_ref[l] + sizes_ref[l] - base for l in range(layers)]
-    own_low = [jnp.maximum(v, off) for v in low]
-    own_high = [jnp.minimum(v, off + shard) for v in high]
+    low, high, own_low, own_high = [], [], [], []
+
+    def bounds():
+        for copy in tables:
+            copy.wait()
+        for l in range(layers):
+            low.append(offsets_ref[l] - base)
+            high.append(offsets_ref[l] + sizes_ref[l] - base)
+            own_low.append(jnp.maximum(low[l], off))
+            own_high.append(jnp.minimum(high[l], off + shard))
+
     lane1 = lax.broadcasted_iota(jnp.int32, (1, 128), 1)
 
-    def squares(value, first):
+    def squares(value, first, lows, highs):
         def add(t, accs):
             pos = place + t * TILE
             v = value(t)
             v = v * v
             return tuple(
                 acc + jnp.where((pos >= lo) & (pos < hi), v, 0.0)
-                for acc, lo, hi in zip(accs, own_low, own_high)
+                for acc, lo, hi in zip(accs, lows, highs)
             )
 
         accs = lax.fori_loop(
@@ -327,18 +394,19 @@
             signal_z(ready.at[j - 1], (c,))
         send_distance(j)
 
-    for op in RS.split():
+    for op in RS:
         i = int(op[1:] or 0) if op != "bar" and op != "mv" else 0
         zt = order[i - 1]
         if op == "bar":
             pl.semaphore_wait(barrier, 5 + 2 * n_z)
             signal_z(ready.at[0], (c,))
         elif op == "mv":
+            bounds()
             for j, ref in enumerate((m_in, v_in)):
                 window(j, ref)
-            wrow[...] = squares(lambda t: mv[t, 0], 0)
+            wrow[...] = squares(lambda t: mv[t, 0], 0, own_low, own_high)
         elif op[0] == "k":
-            pack(zt)
+            pack(i)
         elif op[0] == "A":
             send_raw(zt, 0)
         elif op[0] == "B":
@@ -367,12 +435,20 @@
     for t in range(hz):
         acc = zs[x * 2 + y, t] + rz2[0, t]
         grad_buf[hxy + t] = (acc + (rz2[1, t] + rz2[2, t])) / n
-
-    stats[d] = squares(lambda t: grad_buf[t], layers) + wrow[...]
-
-    @pl.loop(1, n, unroll=True)
-    def _(q):
-        remote(stats.at[d], stats.at[d], send_s, got_s, dev((d + q) % n)).start()
+    grad_buf[step] = jnp.zeros((8, 128), jnp.float32)
+
+    @pl.when(d == n - 1)
+    def _():
+        landed(re2, got_e2)
+        grad_buf[step] = (ze[0] + re2[0] + (re2[1] + re2[2])) / n
+
+    stats[d] = squares(lambda t: grad_buf[t], layers, low, high) + wrow[...]
+
+    for k in range(n_out - 1, -1, -1):
+        for q in range(plane - 1, -1, -1):
+            if k + q > 0:
+                peer = flip(z, k) * plane + flip(p, q)
+                remote(stats.at[d], stats.at[d], send_s, got_s, dev(peer)).start()
 
     halo_copy = remote(mv.at[span - 1], halo, halo_sem.at[0], halo_sem.at[1], dev((d + 1) % n))
     halo_copy.start()
@@ -394,8 +470,7 @@
     for j in range(2):
         mv[0, j] = jnp.where(place < off, halo[j], mv[0, j])
 
-    @pl.loop(0, span)
-    def _(t):
+    def update(t):
         pos = place + t * TILE
         trust_pos = jnp.zeros((8, 128), jnp.float32)
         decay_pos = jnp.zeros((8, 128), jnp.float32)
@@ -408,22 +483,54 @@
         nm = m - nv
         nvw[t] = nv
         nmw[t] = nm
-        ags[d, t] = nm.astype(jnp.bfloat16)
-
-    def block(zz, xx, cc, yy):
-        return zz * plane + xx * 4 + cc * 2 + yy
-
-    def forward(b, device, lo=0, size=span):
-        piece = ags.at[b, pl.ds(lo, size)]
-        remote(piece, piece, send4, got4.at[b], device).start()
-
-    def arrived(b):
-        landed(ags.at[b], got4.at[b])
+        return nm.astype(jnp.bfloat16)
+
+    def zslot(zz, xx, cc, yy):
+        return (cc * n_out + zz) * 4 + xx * 2 + yy
 
     x_side = at(z, 1 - x, c, y)
     y_side = at(z, x, c, 1 - y)
     across = at(z, 1 - x, c, 1 - y)
     partner = at(z, x, 1 - c, y)
+    mine = zslot(z, x, c, y)
+    for t in range(hz):
+        agz[mine, t] = update(hxy + t)
+    for device in (across, x_side, y_side):
+        remote(agz.at[mine], agz.at[mine], send_g, got_in, device).start()
+
+    @pl.loop(0, hxy)
+    def _(t):
+        ags[d, t] = update(t)
+
+    def send_edge():
+        for i, ref in enumerate((nmw, nvw)):
+            remote(ref.at[0], ref.at[step], back_sem.at[i], back_sem.at[2 + i], dev(d - 1)).start()
+
+    def block(zz, xx, cc, yy):
+        return zz * plane + xx * 4 + cc * 2 + yy
+
+    def forward(b, device, lo=0, size=hxy):
+        piece = ags.at[b, pl.ds(lo, size)]
+        remote(piece, piece, send4, got4.at[b], device).start()
+
+    def arrived(b):
+        landed(ags.at[b], got4.at[b])
+
+    def group(cc, zz):
+        return agz.at[pl.ds((cc * n_out + zz) * 4, 4)]
+
+    def z_share():
+        landed(agz.at[pl.ds(0, 3)], got_in)
+        row = group(c, z)
+        for k in ZSEND:
+            remote(row, row, send_g, got_gz.at[z], at(flip(z, k), x, c, y)).start()
+        remote(row, row, send_g, got_gc, partner).start()
+
+    def z_arrived(k):
+        row = group(c, flip(z, k))
+        landed(row, got_gz.at[flip(z, k)])
+        remote(row, row, send_g, got_gc, partner).start()
+
     for k in ZSEND:
         forward(d, at(flip(z, k), x, c, y))
 
@@ -437,14 +544,15 @@
             forward(b, across)
         forward(b, partner)
 
-    def sides(k):
-        zz = flip(z, k)
-        b = block(zz, x, c, 1 - y)
+    def from_y(k):
+        b = block(flip(z, k), x, c, 1 - y)
         arrived(b)
         if k not in DIRECT:
             forward(b, x_side, 0, half_a)
         forward(b, partner)
-        b = block(zz, 1 - x, c, y)
+
+    def from_x(k):
+        b = block(flip(z, k), 1 - x, c, y)
         arrived(b)
         if k not in DIRECT:
             forward(b, y_side, half_a, half_b)
@@ -455,21 +563,64 @@
         arrived(b)
         forward(b, partner)
 
-    visits = (0,) + ZWAIT
-    column(0)
-    for i, k in enumerate(visits):
-        if i + 1 < n_out:
-            column(visits[i + 1])
-        sides(k)
-        if i > 0:
-            corner(visits[i - 1])
-    corner(visits[-1])
+    def edges():
+        @pl.when(d > 0)
+        def _():
+            send_edge()
+
+        @pl.when(d == n - 1)
+        def _():
+            age[0] = update(step)
+            for q in range(1, n):
+                remote(age, age, send_e, got_e, dev(d - q)).start()
+
+    for op in AG:
+        i = int(op[1:])
+        if op[0] == "c":
+            column(i)
+        elif op[0] == "x":
+            from_x(i)
+        elif op[0] == "y":
+            from_y(i)
+        elif op[0] == "d":
+            corner(i)
+        elif op[0] == "g":
+            z_share()
+        elif op[0] == "h":
+            z_arrived(i)
+        elif op[0] == "e":
+            edges()
 
     @pl.loop(0, n_out)
     def _(k):
         for xx in range(2):
             for yy in range(2):
                 arrived(block(k, xx, 1 - c, yy))
+
+    landed(agz.at[pl.ds((1 - c) * (4 * n_out), 4 * n_out)], got_gc)
+
+    @pl.when(d < n - 1)
+    def _():
+        landed(age, got_e)
+        for i, ref in enumerate((nmw, nvw)):
+            landed(ref.at[step], back_sem.at[2 + i])
+
+    @pl.when(d == n - 1)
+    def _():
+        landed(ags.at[pl.ds(0, n - 1), 0], send_e)
+
+    @pl.when(d > 0)
+    def _():
+        for i, ref in enumerate((nmw, nvw)):
+            landed(ref.at[step], back_sem.at[i])
+
+    @pl.when((z != last) | (c != 1))
+    def _():
+        landed(re1.at[pl.ds(0, 1)], send_e1)
+
+    @pl.when((z == last) & (c == 1) & (x * 2 + y < 3))
+    def _():
+        landed(ze, send_e2)
 
     for ref, sem in (
         (r1x, send1x),
@@ -481,27 +632,41 @@
         (recv3.at[pl.ds(0, n_out - 1)], send3),
         (stats.at[pl.ds(0, n - 1)], send_s),
         (ags.at[pl.ds(0, n - 1)], send4),
+        (agz.at[pl.ds(0, n - 1)], send_g),
     ):
         landed(ref, sem)
 
 
-def finish(plan, ags, nmw, nvw, out_ref, nm_ref, nv_ref, nm_out, nv_out, out_sem, own_sem):
-    n, n_spa, shard, step, span = plan
+def finish(
+    plan,
+    ags,
+    agz,
+    age,
+    nmw,
+    nvw,
+    out_ref,
+    nm_ref,
+    nv_ref,
+    nm_out,
+    nv_out,
+    out_sem,
+    own_sem,
+):
+    n, n_spa, shard, step, span, hz = plan
     rows = span * 8
     whole = step * TILE
+    hxy = step - hz
+    pieces = []
+    for b in range(n):
+        zz, xx, cc, yy = b // 8, b // 4 % 2, b // 2 % 2, b % 2
+        slot = (cc * (n // 8) + zz) * 4 + xx * 2 + yy
+        pieces.append((ags.at[b], b * step, hxy))
+        pieces.append((agz.at[slot], b * step + hxy, hz))
+    pieces.append((age, n * step, 1))
     copies = [
-        pltpu.make_async_copy(
-            ags.at[b, pl.ds(0, step)], out_ref.at[pl.ds(b * step, step)], out_sem.at[b]
-        )
-        for b in range(n)
+        pltpu.make_async_copy(src, out_ref.at[pl.ds(first, size)], out_sem.at[i])
+        for i, (src, first, size) in enumerate(pieces)
     ]
-    copies.append(
-        pltpu.make_async_copy(
-            ags.at[n - 1, pl.ds(step, span - step)],
-            out_ref.at[pl.ds(n * step, span - step)],
-            out_sem.at[n],
-        )
-    )
     for copy in copies:
         copy.start()
     d = lax.axis_index("replica") * n_spa + lax.axis_index("spatial")
@@ -536,24 +701,28 @@
     chunk = (plane - 1) * step + span
     tiles = params // TILE
     hz = ZTILES
-    hx = (span - hz + 1) // 2
-    hy = span - hz - hx
+    hx = (step - hz + 1) // 2
+    hy = step - hz - hx
     plan = (n_out, shard, step, span, layers, hx, hy, hz)
     vmem = pl.BlockSpec(memory_space=pltpu.VMEM)
-    smem = pl.BlockSpec(memory_space=pltpu.SMEM)
     anywhere = pl.BlockSpec(memory_space=pltpu.HBM)
     f32, bf16 = jnp.float32, jnp.bfloat16
     dma = pltpu.SemaphoreType.DMA
-    ags, nmw, nvw = pl.pallas_call(
+    ags, agz, age, nmw, nvw = pl.pallas_call(
         functools.partial(kernel, plan),
         out_shape=(
-            pltpu.VMEM((n, span, 8, 128), bf16),
+            pltpu.VMEM((n, hx + hy, 8, 128), bf16),
+            pltpu.VMEM((n, hz, 8, 128), bf16),
+            pltpu.VMEM((1, 8, 128), bf16),
             pltpu.VMEM((span, 8, 128), f32),
             pltpu.VMEM((span, 8, 128), f32),
         ),
-        in_specs=[anywhere, anywhere, anywhere, smem, smem, smem],
-        out_specs=(vmem, vmem, vmem),
+        in_specs=[anywhere] * 6,
+        out_specs=(vmem,) * 5,
         scratch_shapes=[
+            pltpu.SMEM((layers,), jnp.int32),
+            pltpu.SMEM((layers,), jnp.int32),
+            pltpu.SMEM((layers,), jnp.int32),
             pltpu.VMEM((shard,), f32),
             pltpu.VMEM((shard,), f32),
             pltpu.VMEM((n_out, 1, chunk * TILE), bf16),
@@ -567,6 +736,9 @@
             pltpu.VMEM((2 * n_out, 4, hz, 8, 128), bf16),
             pltpu.VMEM((4, hz, 8, 128), f32),
             pltpu.VMEM((3, hz, 8, 128), f32),
+            pltpu.VMEM((2 * n_out, 8, 128), bf16),
+            pltpu.VMEM((1, 8, 128), f32),
+            pltpu.VMEM((3, 8, 128), f32),
             pltpu.VMEM((n_out, hx + hy, 8, 128), f32),
             pltpu.VMEM((n_out, hx + hy, 8, 128), f32),
             pltpu.VMEM((span, 2, 8, 128), f32),
@@ -576,6 +748,7 @@
             pltpu.VMEM((n, 1, 128), f32),
             dma((n_out,)),
             dma((2,)),
+            dma((3,)),
             pltpu.SemaphoreType.REGULAR((n_out,)),
             dma(()),
             dma((2, n_out)),
@@ -591,33 +764,44 @@
             dma(()),
             dma(()),
             dma(()),
+            dma(()),
+            dma(()),
+            dma(()),
+            dma(()),
             dma((2,)),
             dma(()),
             dma(()),
             dma(()),
             dma((n,)),
+            dma(()),
+            dma(()),
+            dma((n_out,)),
+            dma(()),
+            dma(()),
+            dma(()),
+            dma((4,)),
         ],
         compiler_params=pltpu.CompilerParams(
             collective_id=0, has_side_effects=True, vmem_limit_bytes=61 * 2**20
         ),
     )(grads, master, velocity, layer_offsets, layer_sizes, lars_skip)
     weights, nm, nv = pl.pallas_call(
-        functools.partial(finish, (n, n_spa, shard, step, span)),
+        functools.partial(finish, (n, n_spa, shard, step, span, hz)),
         out_shape=(
             jax.ShapeDtypeStruct((tiles, 8, 128), bf16),
             jax.ShapeDtypeStruct((shard,), f32),
             jax.ShapeDtypeStruct((shard,), f32),
         ),
-        in_specs=[vmem, vmem, vmem],
+        in_specs=[vmem] * 5,
         out_specs=(anywhere, anywhere, anywhere),
         scratch_shapes=[
             pltpu.VMEM((shard,), f32),
             pltpu.VMEM((shard,), f32),
-            dma((n + 1,)),
+            dma((2 * n + 1,)),
             dma((2,)),
         ],
         compiler_params=pltpu.CompilerParams(vmem_limit_bytes=16 * 2**20),
-    )(ags, nmw, nvw)
+    )(ags, agz, age, nmw, nvw)
     return weights.reshape(params), nm, nv
 
 

time: 44.3 us -> 42.8 us (0.966)
  Pallas kernels: 43.5 us -> 42 us
    pallas_call x1, Pallas kernels: 41.9 us -> 40.1 us  [windowed(): pl.pallas_call(functools.partial(kernel, plan), out_shape=(pltpu.VMEM((n,...]
where the time goes in v3:
time: 42.8 us; the launch traced here: 42.6 us
  Pallas kernels  42 us (98%)
  between operations  0.64 us (1%)
    pallas_call x1, Pallas kernels, windowed(): pl.pallas_call(functools.partial(kernel, plan), out_shape=(pltpu.VMEM((n,...  40.1 us
    pallas_call x1, Pallas kernels, windowed(): pl.pallas_call(functools.partial(finish, (n, n_spa, shard, step, span, hz...  1.87 us

profile of v3, /device:TPU:0, one launch (start us, length us, event | category | flops | bytes accessed | tf_op | source)
XLA Modules:
  0.0 42.6 jit_solution(3627799611401296902)
XLA Ops:
  0.6 40.1 %shard_map.85 = (bf16[32,21,8,128]{3,2,1,0:T(8,128)(2,1)S(1)}, bf16[32,5,8,128]{3,2,1,0:T(8,128)(2,1)S(1)}, bf16[1,8,128]{2,1,0:T(8,128)(2,1)S(1)}, f32[27,8,128]{2,1,0:T(8,128)S(1)}, f32[27,8,128]{2,1,0:T(8,128)S(1)}) custom-call(bf16[1,1,852992]{2,1,0:T(2,128)(2,1)} %grads_ref.1, f32[26656]{0:T(1024)} %m_ref.1, f32[26656]{0:T(1024)} %v_ref.1, ...), custom_call_target="tpu_custom_call" | custom-call | tf_op jit(solution)/shard_map/pallas_call | solution.py:711
  40.7 1.9 %shard_map.86 = (bf16[833,8,128]{2,1,0:T(8,128)(2,1)}, f32[26656]{0:T(1024)}, f32[26656]{0:T(1024)}) custom-call(bf16[32,21,8,128]{3,2,1,0:T(8,128)(2,1)S(1)} %get-tuple-element.11.ags, bf16[32,5,8,128]{3,2,1,0:T(8,128)(2,1)S(1)} %get-tuple-element.12.agz, bf16[1,8,128]{2,1,0:T(8,128)(2,1)S(1)} %get-tuple-element.13.age, ...), custom_call_target="tpu_custom_call" | custom-call | tf_op jit(solution)/shard_map/pallas_call | solution.py:788

commit v4 on v3

--- a/solution.py
+++ b/solution.py
@@ -9,7 +9,8 @@
 
 MESH = pl.DeviceIdType.MESH
 TILE = 1024
-ZTILES = 5
+ZTILES = 4
+PIECES = 8
 XOR = (2, 3, 1, 0)
 RS = (
     "k1", "bar", "A1", "B1", "k2", "A2", "k3", "k4", "z1", "z2", "z3", "mv", "s1", "B2", "A3",
@@ -41,7 +42,6 @@
     sizes_in,
     skip_in,
     ags,
-    agz,
     age,
     nmw,
     nvw,
@@ -69,6 +69,9 @@
     mv,
     halo,
     grad_buf,
+    layer_of,
+    nvw_pre,
+    step_pre,
     wrow,
     stats,
     in_sem,
@@ -366,7 +369,7 @@
 
     lane1 = lax.broadcasted_iota(jnp.int32, (1, 128), 1)
 
-    def squares(value, first, lows, highs):
+    def squares(value, start, stop, lows, highs, sums=None):
         def add(t, accs):
             pos = place + t * TILE
             v = value(t)
@@ -376,11 +379,13 @@
                 for acc, lo, hi in zip(accs, lows, highs)
             )
 
-        accs = lax.fori_loop(
-            0, span, add, tuple(jnp.zeros((8, 128), jnp.float32) for _ in range(layers))
-        )
+        if sums is None:
+            sums = tuple(jnp.zeros((8, 128), jnp.float32) for _ in range(layers))
+        return lax.fori_loop(start, stop, add, sums)
+
+    def as_row(sums, first):
         row = jnp.zeros((1, 128), jnp.float32)
-        for l, acc in enumerate(accs):
+        for l, acc in enumerate(sums):
             row = jnp.where(lane1 == first + l, jnp.sum(acc, axis=(0, 1), keepdims=True), row)
         return row
 
@@ -404,7 +409,7 @@
             bounds()
             for j, ref in enumerate((m_in, v_in)):
                 window(j, ref)
-            wrow[...] = squares(lambda t: mv[t, 0], 0, own_low, own_high)
+            wrow[...] = as_row(squares(lambda t: mv[t, 0], 0, span, own_low, own_high), 0)
         elif op[0] == "k":
             pack(i)
         elif op[0] == "A":
@@ -423,14 +428,8 @@
                 copy3(zt, z).start()
 
     landed(recv3.at[pl.ds(0, n_out - 1)], got3)
-
-    @pl.loop(0, hxy)
-    def _(t):
-        acc = part[z, t]
-        for k in range(1, n_out):
-            acc = acc + recv3[(z + k) % n_out, t]
-        grad_buf[t] = acc / n
-
+    halo_copy = remote(mv.at[span - 1], halo, halo_sem.at[0], halo_sem.at[1], dev((d + 1) % n))
+    halo_copy.start()
     landed(rz2, gotz2)
     for t in range(hz):
         acc = zs[x * 2 + y, t] + rz2[0, t]
@@ -442,7 +441,17 @@
         landed(re2, got_e2)
         grad_buf[step] = (ze[0] + re2[0] + (re2[1] + re2[2])) / n
 
-    stats[d] = squares(lambda t: grad_buf[t], layers, low, high) + wrow[...]
+    def total_grad(t):
+        acc = part[z, t]
+        for k in range(1, n_out):
+            acc = acc + recv3[(z + k) % n_out, t]
+        acc = acc / n
+        grad_buf[t] = acc
+        return acc
+
+    sums = squares(total_grad, 0, hxy, low, high)
+    sums = squares(lambda t: grad_buf[t], hxy, span, low, high, sums)
+    stats[d] = as_row(sums, layers) + wrow[...]
 
     for k in range(n_out - 1, -1, -1):
         for q in range(plane - 1, -1, -1):
@@ -450,53 +459,65 @@
                 peer = flip(z, k) * plane + flip(p, q)
                 remote(stats.at[d], stats.at[d], send_s, got_s, dev(peer)).start()
 
-    halo_copy = remote(mv.at[span - 1], halo, halo_sem.at[0], halo_sem.at[1], dev((d + 1) % n))
-    halo_copy.start()
-
-    landed(stats.at[pl.ds(0, n - 1)], got_s)
-    total = jnp.sum(stats[...], axis=0)
-    trust, decay = [], []
+    skip_row = jnp.zeros((1, 128), jnp.float32)
     for l in range(layers):
-        wsq = jnp.sum(jnp.where(lane1 == l, total, 0.0), axis=(0, 1), keepdims=True)
-        gsq = jnp.sum(jnp.where(lane1 == layers + l, total, 0.0), axis=(0, 1), keepdims=True)
-        wnorm = jnp.sqrt(jnp.broadcast_to(wsq, (8, 128)))
-        gnorm = jnp.sqrt(jnp.broadcast_to(gsq, (8, 128)))
-        skipped = skip_ref[l].astype(jnp.float32)
-        ratio = 0.02 * wnorm / (gnorm + 0.001 * wnorm + 1e-06)
-        trust.append(skipped + (1.0 - skipped) * ratio)
-        decay.append((1.0 - skipped) * 0.001)
+        skip_row = jnp.where(lane1 == l, skip_ref[l].astype(jnp.float32), skip_row)
+
+    def prepare(t):
+        pos = place + t * TILE
+        which = jnp.zeros((8, 128), jnp.int32)
+        decay = jnp.zeros((8, 128), jnp.float32)
+        for l in range(layers):
+            inside = (pos >= low[l]) & (pos < high[l])
+            which = jnp.where(inside, l, which)
+            decay = jnp.where(inside, (1.0 - skip_ref[l].astype(jnp.float32)) * 0.001, decay)
+        layer_of[t] = which
+        nvw_pre[t] = 0.9 * mv[t, 1]
+        step_pre[t] = 8.0 * (grad_buf[t] + decay * mv[t, 0])
+
+    @pl.loop(1, span)
+    def _(t):
+        prepare(t)
 
     halo_copy.wait()
     for j in range(2):
         mv[0, j] = jnp.where(place < off, halo[j], mv[0, j])
+    prepare(0)
+
+    landed(stats.at[pl.ds(0, n - 1)], got_s)
+    norms = jnp.sqrt(jnp.sum(stats[...], axis=0))
+    wnorm = jnp.broadcast_to(norms, (8, 128))
+    gnorm = pltpu.roll(wnorm, 128 - layers, 1)
+    ratio = 0.02 * wnorm / (gnorm + 0.001 * wnorm + 1e-06)
+    trust_row = skip_row + (1.0 - skip_row) * ratio
+    trust = [
+        jnp.sum(jnp.where(lane1 == l, trust_row, 0.0), axis=1, keepdims=True)
+        for l in range(layers)
+    ]
 
     def update(t):
-        pos = place + t * TILE
-        trust_pos = jnp.zeros((8, 128), jnp.float32)
-        decay_pos = jnp.zeros((8, 128), jnp.float32)
-        for l in range(layers):
-            inside = (pos >= low[l]) & (pos < high[l])
-            trust_pos = jnp.where(inside, trust[l], trust_pos)
-            decay_pos = jnp.where(inside, decay[l], decay_pos)
-        m = mv[t, 0]
-        nv = 0.9 * mv[t, 1] + 8.0 * trust_pos * (grad_buf[t] + decay_pos * m)
-        nm = m - nv
+        which = layer_of[t]
+        trust_pos = jnp.broadcast_to(trust[0], (8, 128))
+        for l in range(1, layers):
+            trust_pos = jnp.where(which == l, trust[l], trust_pos)
+        nv = nvw_pre[t] + trust_pos * step_pre[t]
+        nm = mv[t, 0] - nv
         nvw[t] = nv
         nmw[t] = nm
         return nm.astype(jnp.bfloat16)
-
-    def zslot(zz, xx, cc, yy):
-        return (cc * n_out + zz) * 4 + xx * 2 + yy
 
     x_side = at(z, 1 - x, c, y)
     y_side = at(z, x, c, 1 - y)
     across = at(z, 1 - x, c, 1 - y)
     partner = at(z, x, 1 - c, y)
-    mine = zslot(z, x, c, y)
+
+    def share(b):
+        return ags.at[b, pl.ds(hxy, hz)]
+
     for t in range(hz):
-        agz[mine, t] = update(hxy + t)
+        ags[d, hxy + t] = update(hxy + t)
     for device in (across, x_side, y_side):
-        remote(agz.at[mine], agz.at[mine], send_g, got_in, device).start()
+        remote(share(d), share(d), send_g, got_in, device).start()
 
     @pl.loop(0, hxy)
     def _(t):
@@ -514,22 +535,25 @@
         remote(piece, piece, send4, got4.at[b], device).start()
 
     def arrived(b):
-        landed(ags.at[b], got4.at[b])
-
-    def group(cc, zz):
-        return agz.at[pl.ds((cc * n_out + zz) * 4, 4)]
+        landed(ags.at[b, pl.ds(0, hxy)], got4.at[b])
+
+    def tiles(count):
+        return ags.at[pl.ds(0, count), pl.ds(0, hz)]
 
     def z_share():
-        landed(agz.at[pl.ds(0, 3)], got_in)
-        row = group(c, z)
-        for k in ZSEND:
-            remote(row, row, send_g, got_gz.at[z], at(flip(z, k), x, c, y)).start()
-        remote(row, row, send_g, got_gc, partner).start()
+        landed(tiles(3), got_in)
+        for j in range(4):
+            b = block(z, j // 2, c, j % 2)
+            for k in ZSEND:
+                peer = at(flip(z, k), x, c, y)
+                remote(share(b), share(b), send_g, got_gz.at[z], peer).start()
+            remote(share(b), share(b), send_g, got_gc, partner).start()
 
     def z_arrived(k):
-        row = group(c, flip(z, k))
-        landed(row, got_gz.at[flip(z, k)])
-        remote(row, row, send_g, got_gc, partner).start()
+        landed(tiles(4), got_gz.at[flip(z, k)])
+        for j in range(4):
+            b = block(flip(z, k), j // 2, c, j % 2)
+            remote(share(b), share(b), send_g, got_gc, partner).start()
 
     for k in ZSEND:
         forward(d, at(flip(z, k), x, c, y))
@@ -597,7 +621,7 @@
             for yy in range(2):
                 arrived(block(k, xx, 1 - c, yy))
 
-    landed(agz.at[pl.ds((1 - c) * (4 * n_out), 4 * n_out)], got_gc)
+    landed(tiles(4 * n_out), got_gc)
 
     @pl.when(d < n - 1)
     def _():
@@ -631,8 +655,8 @@
         (rz2, sendz2),
         (recv3.at[pl.ds(0, n_out - 1)], send3),
         (stats.at[pl.ds(0, n - 1)], send_s),
-        (ags.at[pl.ds(0, n - 1)], send4),
-        (agz.at[pl.ds(0, n - 1)], send_g),
+        (ags.at[pl.ds(0, n - 1), pl.ds(0, hxy)], send4),
+        (tiles(n - 1), send_g),
     ):
         landed(ref, sem)
 
@@ -640,7 +664,6 @@
 def finish(
     plan,
     ags,
-    agz,
     age,
     nmw,
     nvw,
@@ -652,21 +675,19 @@
     out_sem,
     own_sem,
 ):
-    n, n_spa, shard, step, span, hz = plan
+    n, n_spa, shard, step, span = plan
     rows = span * 8
     whole = step * TILE
-    hxy = step - hz
-    pieces = []
-    for b in range(n):
-        zz, xx, cc, yy = b // 8, b // 4 % 2, b // 2 % 2, b % 2
-        slot = (cc * (n // 8) + zz) * 4 + xx * 2 + yy
-        pieces.append((ags.at[b], b * step, hxy))
-        pieces.append((agz.at[slot], b * step + hxy, hz))
-    pieces.append((age, n * step, 1))
+    part = n * step // PIECES
     copies = [
-        pltpu.make_async_copy(src, out_ref.at[pl.ds(first, size)], out_sem.at[i])
-        for i, (src, first, size) in enumerate(pieces)
+        pltpu.make_async_copy(
+            ags.at[pl.ds(i * part, part)], out_ref.at[pl.ds(i * part, part)], out_sem.at[i]
+        )
+        for i in range(PIECES)
     ]
+    copies.append(
+        pltpu.make_async_copy(age, out_ref.at[pl.ds(n * step, 1)], out_sem.at[PIECES])
+    )
     for copy in copies:
         copy.start()
     d = lax.axis_index("replica") * n_spa + lax.axis_index("spatial")
@@ -708,17 +729,16 @@
     anywhere = pl.BlockSpec(memory_space=pltpu.HBM)
     f32, bf16 = jnp.float32, jnp.bfloat16
     dma = pltpu.SemaphoreType.DMA
-    ags, agz, age, nmw, nvw = pl.pallas_call(
+    ags, age, nmw, nvw = pl.pallas_call(
         functools.partial(kernel, plan),
         out_shape=(
-            pltpu.VMEM((n, hx + hy, 8, 128), bf16),
-            pltpu.VMEM((n, hz, 8, 128), bf16),
+            pltpu.VMEM((n, step, 8, 128), bf16),
             pltpu.VMEM((1, 8, 128), bf16),
             pltpu.VMEM((span, 8, 128), f32),
             pltpu.VMEM((span, 8, 128), f32),
         ),
         in_specs=[anywhere] * 6,
-        out_specs=(vmem,) * 5,
+        out_specs=(vmem,) * 4,
         scratch_shapes=[
             pltpu.SMEM((layers,), jnp.int32),
             pltpu.SMEM((layers,), jnp.int32),
@@ -744,6 +764,9 @@
             pltpu.VMEM((span, 2, 8, 128), f32),
             pltpu.VMEM((2, 8, 128), f32),
             pltpu.VMEM((span, 8, 128), f32),
+            pltpu.VMEM((span, 8, 128), jnp.int32),
+            pltpu.VMEM((span, 8, 128), f32),
+            pltpu.VMEM((span, 8, 128), f32),
             pltpu.VMEM((1, 128), f32),
             pltpu.VMEM((n, 1, 128), f32),
             dma((n_out,)),
@@ -786,22 +809,22 @@
         ),
     )(grads, master, velocity, layer_offsets, layer_sizes, lars_skip)
     weights, nm, nv = pl.pallas_call(
-        functools.partial(finish, (n, n_spa, shard, step, span, hz)),
+        functools.partial(finish, (n, n_spa, shard, step, span)),
         out_shape=(
             jax.ShapeDtypeStruct((tiles, 8, 128), bf16),
             jax.ShapeDtypeStruct((shard,), f32),
             jax.ShapeDtypeStruct((shard,), f32),
         ),
-        in_specs=[vmem] * 5,
+        in_specs=[vmem] * 4,
         out_specs=(anywhere, anywhere, anywhere),
         scratch_shapes=[
             pltpu.VMEM((shard,), f32),
             pltpu.VMEM((shard,), f32),
-            dma((2 * n + 1,)),
+            dma((PIECES + 1,)),
             dma((2,)),
         ],
         compiler_params=pltpu.CompilerParams(vmem_limit_bytes=16 * 2**20),
-    )(ags, agz, age, nmw, nvw)
+    )(ags.reshape(n * step, 8, 128), age, nmw, nvw)
     return weights.reshape(params), nm, nv
 
 

time: 42.8 us -> 41.2 us (0.963)
  Pallas kernels: 42 us -> 40.4 us
    pallas_call x1, Pallas kernels: 40.1 us -> 39.1 us  [windowed(): pl.pallas_call(functools.partial(kernel, plan), out_shape=(pltpu.VMEM((n,...]
    pallas_call x1, Pallas kernels: 1.87 us -> 1.36 us  [windowed(): pl.pallas_call(functools.partial(finish, (n, n_spa, shard, step, span)),...]
where the time goes in v4:
time: 41.2 us; the launch traced here: 41.1 us
  Pallas kernels  40.4 us (98%)
  between operations  0.64 us (2%)
    pallas_call x1, Pallas kernels, windowed(): pl.pallas_call(functools.partial(kernel, plan), out_shape=(pltpu.VMEM((n,...  39.1 us
    pallas_call x1, Pallas kernels, windowed(): pl.pallas_call(functools.partial(finish, (n, n_spa, shard, step, span)),...  1.36 us

profile of v4, /device:TPU:0, one launch (start us, length us, event | category | flops | bytes accessed | tf_op | source)
XLA Modules:
  0.0 41.1 jit_solution(454167530443246107)
XLA Ops:
  0.6 39.1 %shard_map.85 = (bf16[32,26,8,128]{3,2,1,0:T(8,128)(2,1)S(1)}, bf16[1,8,128]{2,1,0:T(8,128)(2,1)S(1)}, f32[27,8,128]{2,1,0:T(8,128)S(1)}, f32[27,8,128]{2,1,0:T(8,128)S(1)}) custom-call(bf16[1,1,852992]{2,1,0:T(2,128)(2,1)} %grads_ref.1, f32[26656]{0:T(1024)} %m_ref.1, f32[26656]{0:T(1024)} %v_ref.1, s32[6]{0:T(128)} %offsets_in.1, s32[6]{0:T(128)} %sizes_in.1, ...), custom_call_target="tpu_custom_call" | custom-call | tf_op jit(solution)/shard_map/pallas_call | solution.py:732
  39.7 1.4 %shard_map.86 = (bf16[833,8,128]{2,1,0:T(8,128)(2,1)}, f32[26656]{0:T(1024)}, f32[26656]{0:T(1024)}) custom-call(bf16[832,8,128]{2,1,0:T(8,128)(2,1)S(1)} %bitcast.2, bf16[1,8,128]{2,1,0:T(8,128)(2,1)S(1)} %get-tuple-element.11.age, f32[27,8,128]{2,1,0:T(8,128)S(1)} %get-tuple-element.12.nmw, f32[27,8,128]{2,1,0:T(8,128)S(1)} %get-tuple-element.13.nvw), custom_call_target="tpu_custom_call" | custom-call | tf_op jit(solution)/shard_map/pallas_call | solution.py:811

commit v5 on v4

--- a/solution.py
+++ b/solution.py
@@ -10,18 +10,18 @@
 MESH = pl.DeviceIdType.MESH
 TILE = 1024
 ZTILES = 4
+SHARE = 6
 PIECES = 8
-XOR = (2, 3, 1, 0)
 RS = (
     "k1", "bar", "A1", "B1", "k2", "A2", "k3", "k4", "z1", "z2", "z3", "mv", "s1", "B2", "A3",
-    "s2", "p1", "B3", "A4", "s3", "p2", "B4", "Z", "s4", "p3", "p4",
+    "s2", "p1", "B3", "A4", "s3", "p2", "B4", "s4", "Z", "p3", "p4",
 )
 ZSEND = (1, 2, 3)
 AG = (
     "c0", "c1", "g0", "x0", "y0", "c2", "e0", "c3", "x1", "y1", "d0", "x2", "y2", "d1", "h1",
     "h2", "h3", "x3", "y3", "d2", "d3",
 )
-DIRECT = (0, 3)
+DIRECT = (0, 1, 2, 3)
 
 
 def flip(i, k):
@@ -116,8 +116,9 @@
     rows = span * 8
     hxy = hx + hy
     last = n_out - 1
-    half_a = (hxy + 1) // 2
-    half_b = hxy - half_a
+    main = step - SHARE
+    half_a = (main + 1) // 2
+    half_b = main - half_a
     r = lax.axis_index("replica")
     y = lax.axis_index("spatial")
     d = r * 2 + y
@@ -142,9 +143,8 @@
             grads_ref.at[0, :, pl.ds(start, chunk * TILE)], gin.at[zt], in_sem.at[zt]
         )
 
-    order = [(z + k) % n_out for k in range(1, n_out + 1)]
-    if XOR:
-        order = [flip(z, k) for k in XOR]
+    h = z // 2
+    order = [3 - 3 * h, 2 - h, flip(z, 1), z]
     for zt in order:
         load(zt).start()
     mv_loads = [
@@ -254,10 +254,12 @@
 
         remote(sy.at[zt], r2y.at[zt], send2y, got2y.at[zt], at(z, 1 - x, c, y)).start()
 
-    def copy3(zt, src):
-        return remote(part.at[zt], recv3.at[src], send3, got3, at(zt, x, c, y))
-
-    def sum_plane(zt):
+    def pass_on(zt, lo, size):
+        rows = pl.ds(lo, size)
+        to = at(zt, x, c, y)
+        remote(part.at[zt, rows], recv3.at[z, rows], send3, got3, to).start()
+
+    def sum_plane(zt, send):
         own = first(x, c, y)
         landed(r1x.at[1, zt], got1x.at[1, zt])
         landed(r2x.at[zt], got2x.at[zt])
@@ -266,12 +268,17 @@
         def _(t):
             part[zt, t] = raws(zt, 1, t, r1x, own) + r2x[zt, t]
 
+        if send:
+            pass_on(zt, 0, hx)
         landed(r1y.at[1, zt], got1y.at[1, zt])
         landed(r2y.at[zt], got2y.at[zt])
 
         @pl.loop(0, hy, unroll=2)
         def _(t):
             part[zt, hx + t] = raws(zt, 1, t, r1y, own + hx) + r2y[zt, t]
+
+        if send:
+            pass_on(zt, hx, hy)
 
     def send_far(zt, other):
         cc = 1 - c if other else c
@@ -423,9 +430,7 @@
         elif op[0] == "s":
             sum_raw(zt)
         elif op[0] == "p":
-            sum_plane(zt)
-            if i < n_out:
-                copy3(zt, z).start()
+            sum_plane(zt, i < n_out)
 
     landed(recv3.at[pl.ds(0, n_out - 1)], got3)
     halo_copy = remote(mv.at[span - 1], halo, halo_sem.at[0], halo_sem.at[1], dev((d + 1) % n))
@@ -512,14 +517,14 @@
     partner = at(z, x, 1 - c, y)
 
     def share(b):
-        return ags.at[b, pl.ds(hxy, hz)]
-
-    for t in range(hz):
-        ags[d, hxy + t] = update(hxy + t)
+        return ags.at[b, pl.ds(main, SHARE)]
+
+    for t in range(main, step):
+        ags[d, t] = update(t)
     for device in (across, x_side, y_side):
         remote(share(d), share(d), send_g, got_in, device).start()
 
-    @pl.loop(0, hxy)
+    @pl.loop(0, main)
     def _(t):
         ags[d, t] = update(t)
 
@@ -530,15 +535,15 @@
     def block(zz, xx, cc, yy):
         return zz * plane + xx * 4 + cc * 2 + yy
 
-    def forward(b, device, lo=0, size=hxy):
+    def forward(b, device, lo=0, size=main):
         piece = ags.at[b, pl.ds(lo, size)]
         remote(piece, piece, send4, got4.at[b], device).start()
 
     def arrived(b):
-        landed(ags.at[b, pl.ds(0, hxy)], got4.at[b])
+        landed(ags.at[b, pl.ds(0, main)], got4.at[b])
 
     def tiles(count):
-        return ags.at[pl.ds(0, count), pl.ds(0, hz)]
+        return ags.at[pl.ds(0, count), pl.ds(0, SHARE)]
 
     def z_share():
         landed(tiles(3), got_in)
@@ -655,7 +660,7 @@
         (rz2, sendz2),
         (recv3.at[pl.ds(0, n_out - 1)], send3),
         (stats.at[pl.ds(0, n - 1)], send_s),
-        (ags.at[pl.ds(0, n - 1), pl.ds(0, hxy)], send4),
+        (ags.at[pl.ds(0, n - 1), pl.ds(0, main)], send4),
         (tiles(n - 1), send_g),
     ):
         landed(ref, sem)
@@ -836,8 +841,7 @@
     return (
         n_spa == 2
         and n_rep % 4 == 0
-        and n_out >= 2
-        and n_out & (n_out - 1) == 0
+        and n_out == 4
         and params % TILE == 0
         and shard >= TILE
         and 0 < n * rest <= TILE

time: 41.2 us -> 40.3 us (0.978)
  Pallas kernels: 40.4 us -> 39.5 us
    pallas_call x1, Pallas kernels: 39.1 us -> 38.1 us  [windowed(): pl.pallas_call(functools.partial(kernel, plan), out_shape=(pltpu.VMEM((n,...]
where the time goes in v5:
time: 40.3 us; the launch traced here: 40.1 us
  Pallas kernels  39.5 us (98%)
  between operations  0.64 us (2%)
    pallas_call x1, Pallas kernels, windowed(): pl.pallas_call(functools.partial(kernel, plan), out_shape=(pltpu.VMEM((n,...  38.1 us
    pallas_call x1, Pallas kernels, windowed(): pl.pallas_call(functools.partial(finish, (n, n_spa, shard, step, span)),...  1.36 us

profile of v5, /device:TPU:0, one launch (start us, length us, event | category | flops | bytes accessed | tf_op | source)
XLA Modules:
  0.0 40.1 jit_solution(5529264562351586066)
XLA Ops:
  0.6 38.1 %shard_map.85 = (bf16[32,26,8,128]{3,2,1,0:T(8,128)(2,1)S(1)}, bf16[1,8,128]{2,1,0:T(8,128)(2,1)S(1)}, f32[27,8,128]{2,1,0:T(8,128)S(1)}, f32[27,8,128]{2,1,0:T(8,128)S(1)}) custom-call(bf16[1,1,852992]{2,1,0:T(2,128)(2,1)} %grads_ref.1, f32[26656]{0:T(1024)} %m_ref.1, f32[26656]{0:T(1024)} %v_ref.1, s32[6]{0:T(128)} %offsets_in.1, s32[6]{0:T(128)} %sizes_in.1, ...), custom_call_target="tpu_custom_call" | custom-call | tf_op jit(solution)/shard_map/pallas_call | solution.py:737
  38.7 1.4 %shard_map.86 = (bf16[833,8,128]{2,1,0:T(8,128)(2,1)}, f32[26656]{0:T(1024)}, f32[26656]{0:T(1024)}) custom-call(bf16[832,8,128]{2,1,0:T(8,128)(2,1)S(1)} %bitcast.2, bf16[1,8,128]{2,1,0:T(8,128)(2,1)S(1)} %get-tuple-element.11.age, f32[27,8,128]{2,1,0:T(8,128)S(1)} %get-tuple-element.12.nmw, f32[27,8,128]{2,1,0:T(8,128)S(1)} %get-tuple-element.13.nvw), custom_call_target="tpu_custom_call" | custom-call | tf_op jit(solution)/shard_map/pallas_call | solution.py:816

commit v6 on v5

--- a/solution.py
+++ b/solution.py
@@ -16,10 +16,12 @@
     "k1", "bar", "A1", "B1", "k2", "A2", "k3", "k4", "z1", "z2", "z3", "mv", "s1", "B2", "A3",
     "s2", "p1", "B3", "A4", "s3", "p2", "B4", "s4", "Z", "p3", "p4",
 )
-ZSEND = (1, 2, 3)
+ZSEND = "mfn"
+VISIT = "mnf"
+COLUMN = "axyp"
 AG = (
-    "c0", "c1", "g0", "x0", "y0", "c2", "e0", "c3", "x1", "y1", "d0", "x2", "y2", "d1", "h1",
-    "h2", "h3", "x3", "y3", "d2", "d3",
+    "c0", "c1", "g0", "c2", "x0", "y0", "c3", "e0", "x1", "y1", "d0", "x2", "y2", "d1", "x3",
+    "y3", "d2", "h1", "h2", "h3", "d3",
 )
 DIRECT = (0, 1, 2, 3)
 
@@ -542,6 +544,10 @@
     def arrived(b):
         landed(ags.at[b, pl.ds(0, main)], got4.at[b])
 
+    zone = {"m": flip(z, 1), "n": 2 - h, "f": 3 - 3 * h}
+    visits = [z] + [zone[k] for k in VISIT]
+    sends = [zone[k] for k in ZSEND]
+
     def tiles(count):
         return ags.at[pl.ds(0, count), pl.ds(0, SHARE)]
 
@@ -549,46 +555,50 @@
         landed(tiles(3), got_in)
         for j in range(4):
             b = block(z, j // 2, c, j % 2)
-            for k in ZSEND:
-                peer = at(flip(z, k), x, c, y)
+            for to in sends:
+                peer = at(to, x, c, y)
                 remote(share(b), share(b), send_g, got_gz.at[z], peer).start()
             remote(share(b), share(b), send_g, got_gc, partner).start()
 
     def z_arrived(k):
-        landed(tiles(4), got_gz.at[flip(z, k)])
+        landed(tiles(4), got_gz.at[visits[k]])
         for j in range(4):
-            b = block(flip(z, k), j // 2, c, j % 2)
+            b = block(visits[k], j // 2, c, j % 2)
             remote(share(b), share(b), send_g, got_gc, partner).start()
 
-    for k in ZSEND:
-        forward(d, at(flip(z, k), x, c, y))
+    for to in sends:
+        forward(d, at(to, x, c, y))
 
     def column(k):
-        b = block(flip(z, k), x, c, y)
+        b = block(visits[k], x, c, y)
         if k > 0:
             arrived(b)
-        forward(b, x_side)
-        forward(b, y_side)
-        if k in DIRECT:
-            forward(b, across)
-        forward(b, partner)
+        for way in COLUMN:
+            if way == "x":
+                forward(b, x_side)
+            elif way == "y":
+                forward(b, y_side)
+            elif way == "p":
+                forward(b, partner)
+            elif k in DIRECT:
+                forward(b, across)
 
     def from_y(k):
-        b = block(flip(z, k), x, c, 1 - y)
+        b = block(visits[k], x, c, 1 - y)
         arrived(b)
         if k not in DIRECT:
             forward(b, x_side, 0, half_a)
         forward(b, partner)
 
     def from_x(k):
-        b = block(flip(z, k), 1 - x, c, y)
+        b = block(visits[k], 1 - x, c, y)
         arrived(b)
         if k not in DIRECT:
             forward(b, y_side, half_a, half_b)
         forward(b, partner)
 
     def corner(k):
-        b = block(flip(z, k), 1 - x, c, 1 - y)
+        b = block(visits[k], 1 - x, c, 1 - y)
         arrived(b)
         forward(b, partner)
 

time: 40.3 us -> 40 us (level)
  no operation moved by 1% of the time
where the time goes in v6:
time: 40 us; the launch traced here: 39.8 us
  Pallas kernels  39.2 us (98%)
  between operations  0.64 us (2%)
    pallas_call x1, Pallas kernels, windowed(): pl.pallas_call(functools.partial(kernel, plan), out_shape=(pltpu.VMEM((n,...  37.8 us
    pallas_call x1, Pallas kernels, windowed(): pl.pallas_call(functools.partial(finish, (n, n_spa, shard, step, span)),...  1.36 us

profile of v6, /device:TPU:0, one launch (start us, length us, event | category | flops | bytes accessed | tf_op | source)
XLA Modules:
  0.0 39.8 jit_solution(3032078092650308319)
XLA Ops:
  0.6 37.8 %shard_map.85 = (bf16[32,26,8,128]{3,2,1,0:T(8,128)(2,1)S(1)}, bf16[1,8,128]{2,1,0:T(8,128)(2,1)S(1)}, f32[27,8,128]{2,1,0:T(8,128)S(1)}, f32[27,8,128]{2,1,0:T(8,128)S(1)}) custom-call(bf16[1,1,852992]{2,1,0:T(2,128)(2,1)} %grads_ref.1, f32[26656]{0:T(1024)} %m_ref.1, f32[26656]{0:T(1024)} %v_ref.1, s32[6]{0:T(128)} %offsets_in.1, s32[6]{0:T(128)} %sizes_in.1, ...), custom_call_target="tpu_custom_call" | custom-call | tf_op jit(solution)/shard_map/pallas_call | solution.py:747
  38.5 1.4 %shard_map.86 = (bf16[833,8,128]{2,1,0:T(8,128)(2,1)}, f32[26656]{0:T(1024)}, f32[26656]{0:T(1024)}) custom-call(bf16[832,8,128]{2,1,0:T(8,128)(2,1)S(1)} %bitcast.2, bf16[1,8,128]{2,1,0:T(8,128)(2,1)S(1)} %get-tuple-element.11.age, f32[27,8,128]{2,1,0:T(8,128)S(1)} %get-tuple-element.12.nmw, f32[27,8,128]{2,1,0:T(8,128)S(1)} %get-tuple-element.13.nvw), custom_call_target="tpu_custom_call" | custom-call | tf_op jit(solution)/shard_map/pallas_call | solution.py:826

commit v7 on v6

--- a/solution.py
+++ b/solution.py
@@ -13,15 +13,15 @@
 SHARE = 6
 PIECES = 8
 RS = (
-    "k1", "bar", "A1", "B1", "k2", "A2", "k3", "k4", "z1", "z2", "z3", "mv", "s1", "B2", "A3",
+    "k1", "bar", "A1", "B1", "k2", "A2", "B2", "k3", "k4", "z1", "z2", "z3", "mv", "s1", "A3",
     "s2", "p1", "B3", "A4", "s3", "p2", "B4", "s4", "Z", "p3", "p4",
 )
 ZSEND = "mfn"
 VISIT = "mnf"
 COLUMN = "axyp"
 AG = (
-    "c0", "c1", "g0", "c2", "x0", "y0", "c3", "e0", "x1", "y1", "d0", "x2", "y2", "d1", "x3",
-    "y3", "d2", "h1", "h2", "h3", "d3",
+    "c0", "c1", "g0", "c2", "c3", "x0", "y0", "e0", "x1", "y1", "d0", "x2", "y2", "x3", "y3",
+    "d1", "d2", "h1", "h2", "d3", "h3",
 )
 DIRECT = (0, 1, 2, 3)
 
@@ -392,11 +392,15 @@
             sums = tuple(jnp.zeros((8, 128), jnp.float32) for _ in range(layers))
         return lax.fori_loop(start, stop, add, sums)
 
+    sub8 = lax.broadcasted_iota(jnp.int32, (8, 128), 0)
+    lane8 = lax.broadcasted_iota(jnp.int32, (8, 128), 1)
+
     def as_row(sums, first):
-        row = jnp.zeros((1, 128), jnp.float32)
+        rows8 = jnp.zeros((8, 128), jnp.float32)
         for l, acc in enumerate(sums):
-            row = jnp.where(lane1 == first + l, jnp.sum(acc, axis=(0, 1), keepdims=True), row)
-        return row
+            rows8 = jnp.where(sub8 == l, jnp.sum(acc, axis=0, keepdims=True), rows8)
+        totals = jnp.sum(rows8, axis=1, keepdims=True)
+        return jnp.sum(jnp.where(lane8 == sub8 + first, totals, 0.0), axis=0, keepdims=True)
 
     def step_z(j):
         if j == 1:
@@ -843,7 +847,7 @@
     return weights.reshape(params), nm, nv
 
 
-def tiled(n_rep, n_spa, params):
+def tiled(n_rep, n_spa, params, layers):
     n = n_rep * n_spa
     shard = params // n
     rest = shard % TILE
@@ -852,6 +856,7 @@
         n_spa == 2
         and n_rep % 4 == 0
         and n_out == 4
+        and layers <= 8
         and params % TILE == 0
         and shard >= TILE
         and 0 < n * rest <= TILE
@@ -860,7 +865,7 @@
 
 
 def step_fn(n_rep, n_spa, grads, *rest):
-    if tiled(n_rep, n_spa, grads.shape[2]):
+    if tiled(n_rep, n_spa, grads.shape[2], rest[2].shape[0]):
         return windowed(n_rep, n_spa, grads, *rest)
     return shards(grads, *rest)
 

time: 40 us -> 39.9 us (level)
  no operation moved by 1% of the time
where the time goes in v7:
time: 39.9 us; the launch traced here: 39.7 us
  Pallas kernels  39.1 us (98%)
  between operations  0.64 us (2%)
    pallas_call x1, Pallas kernels, windowed(): pl.pallas_call(functools.partial(kernel, plan), out_shape=(pltpu.VMEM((n,...  37.7 us
    pallas_call x1, Pallas kernels, windowed(): pl.pallas_call(functools.partial(finish, (n, n_spa, shard, step, span)),...  1.36 us

profile of v7, /device:TPU:0, one launch (start us, length us, event | category | flops | bytes accessed | tf_op | source)
XLA Modules:
  0.0 39.7 jit_solution(18202395571544564943)
XLA Ops:
  0.6 37.7 %shard_map.85 = (bf16[32,26,8,128]{3,2,1,0:T(8,128)(2,1)S(1)}, bf16[1,8,128]{2,1,0:T(8,128)(2,1)S(1)}, f32[27,8,128]{2,1,0:T(8,128)S(1)}, f32[27,8,128]{2,1,0:T(8,128)S(1)}) custom-call(bf16[1,1,852992]{2,1,0:T(2,128)(2,1)} %grads_ref.1, f32[26656]{0:T(1024)} %m_ref.1, f32[26656]{0:T(1024)} %v_ref.1, s32[6]{0:T(128)} %offsets_in.1, s32[6]{0:T(128)} %sizes_in.1, ...), custom_call_target="tpu_custom_call" | custom-call | tf_op jit(solution)/shard_map/pallas_call | solution.py:751
  38.4 1.4 %shard_map.86 = (bf16[833,8,128]{2,1,0:T(8,128)(2,1)}, f32[26656]{0:T(1024)}, f32[26656]{0:T(1024)}) custom-call(bf16[832,8,128]{2,1,0:T(8,128)(2,1)S(1)} %bitcast.2, bf16[1,8,128]{2,1,0:T(8,128)(2,1)S(1)} %get-tuple-element.11.age, f32[27,8,128]{2,1,0:T(8,128)S(1)} %get-tuple-element.12.nmw, f32[27,8,128]{2,1,0:T(8,128)S(1)} %get-tuple-element.13.nvw), custom_call_target="tpu_custom_call" | custom-call | tf_op jit(solution)/shard_map/pallas_call | solution.py:830

commit v8 on v7

--- a/solution.py
+++ b/solution.py
@@ -21,7 +21,7 @@
 COLUMN = "axyp"
 AG = (
     "c0", "c1", "g0", "c2", "c3", "x0", "y0", "e0", "x1", "y1", "d0", "x2", "y2", "x3", "y3",
-    "d1", "d2", "h1", "h2", "d3", "h3",
+    "d1", "d2", "h1", "h2", "n0", "d3", "h3",
 )
 DIRECT = (0, 1, 2, 3)
 
@@ -45,6 +45,8 @@
     skip_in,
     ags,
     age,
+    nm_out,
+    nv_out,
     nmw,
     nvw,
     offsets_ref,
@@ -617,6 +619,21 @@
             for q in range(1, n):
                 remote(age, age, send_e, got_e, dev(d - q)).start()
 
+    def own_rows():
+        @pl.when(d < n - 1)
+        def _():
+            for i, ref in enumerate((nmw, nvw)):
+                landed(ref.at[step], back_sem.at[2 + i])
+
+        back_l = 128 - shift_l
+        for src, buf in ((nmw, nm_out), (nvw, nv_out)):
+            w = src[...].reshape(rows, 128)
+            w = pltpu.roll(w, (rows - shift_r) % rows, 0)
+            w = pltpu.roll(w, back_l % 128, 1)
+            w = jnp.where(lane < back_l, w, pltpu.roll(w, rows - 1, 0))
+            buf[pl.ds(0, whole)] = w[: step * 8].reshape(whole)
+            buf[pl.ds(whole, shard - whole)] = w[step * 8, : shard - whole].reshape(shard - whole)
+
     for op in AG:
         i = int(op[1:])
         if op[0] == "c":
@@ -633,6 +650,8 @@
             z_arrived(i)
         elif op[0] == "e":
             edges()
+        elif op[0] == "n":
+            own_rows()
 
     @pl.loop(0, n_out)
     def _(k):
@@ -645,8 +664,6 @@
     @pl.when(d < n - 1)
     def _():
         landed(age, got_e)
-        for i, ref in enumerate((nmw, nvw)):
-            landed(ref.at[step], back_sem.at[2 + i])
 
     @pl.when(d == n - 1)
     def _():
@@ -680,51 +697,17 @@
         landed(ref, sem)
 
 
-def finish(
-    plan,
-    ags,
-    age,
-    nmw,
-    nvw,
-    out_ref,
-    nm_ref,
-    nv_ref,
-    nm_out,
-    nv_out,
-    out_sem,
-    own_sem,
-):
-    n, n_spa, shard, step, span = plan
-    rows = span * 8
-    whole = step * TILE
-    part = n * step // PIECES
+def finish(plan, ags, age, nm, nv, out_ref, nm_ref, nv_ref, sem):
+    part, last = plan
     copies = [
-        pltpu.make_async_copy(
-            ags.at[pl.ds(i * part, part)], out_ref.at[pl.ds(i * part, part)], out_sem.at[i]
-        )
-        for i in range(PIECES)
+        (ags.at[pl.ds(i * part, part)], out_ref.at[pl.ds(i * part, part)]) for i in range(PIECES)
     ]
-    copies.append(
-        pltpu.make_async_copy(age, out_ref.at[pl.ds(n * step, 1)], out_sem.at[PIECES])
-    )
+    copies += [(nm, nm_ref), (nv, nv_ref), (age, out_ref.at[pl.ds(last, 1)])]
+    copies = [
+        pltpu.make_async_copy(src, dst, sem.at[i]) for i, (src, dst) in enumerate(copies)
+    ]
     for copy in copies:
         copy.start()
-    d = lax.axis_index("replica") * n_spa + lax.axis_index("spatial")
-    off = d * (shard - whole)
-    shift_l = off % 128
-    shift_r = off // 128
-    back_l = 128 - shift_l
-    lane = lax.broadcasted_iota(jnp.int32, (rows, 128), 1)
-    for j, (src, buf, ref) in enumerate(((nmw, nm_out, nm_ref), (nvw, nv_out, nv_ref))):
-        x = src[...].reshape(rows, 128)
-        x = pltpu.roll(x, (rows - shift_r) % rows, 0)
-        x = pltpu.roll(x, back_l % 128, 1)
-        x = jnp.where(lane < back_l, x, pltpu.roll(x, rows - 1, 0))
-        buf[pl.ds(0, whole)] = x[: step * 8].reshape(whole)
-        buf[pl.ds(whole, shard - whole)] = x[step * 8, : shard - whole].reshape(shard - whole)
-        copy = pltpu.make_async_copy(buf, ref, own_sem.at[j])
-        copy.start()
-        copies.append(copy)
     for copy in copies:
         copy.wait()
 
@@ -753,12 +736,14 @@
         out_shape=(
             pltpu.VMEM((n, step, 8, 128), bf16),
             pltpu.VMEM((1, 8, 128), bf16),
-            pltpu.VMEM((span, 8, 128), f32),
-            pltpu.VMEM((span, 8, 128), f32),
+            pltpu.VMEM((shard,), f32),
+            pltpu.VMEM((shard,), f32),
         ),
         in_specs=[anywhere] * 6,
         out_specs=(vmem,) * 4,
         scratch_shapes=[
+            pltpu.VMEM((span, 8, 128), f32),
+            pltpu.VMEM((span, 8, 128), f32),
             pltpu.SMEM((layers,), jnp.int32),
             pltpu.SMEM((layers,), jnp.int32),
             pltpu.SMEM((layers,), jnp.int32),
@@ -828,7 +813,7 @@
         ),
     )(grads, master, velocity, layer_offsets, layer_sizes, lars_skip)
     weights, nm, nv = pl.pallas_call(
-        functools.partial(finish, (n, n_spa, shard, step, span)),
+        functools.partial(finish, (n * step // PIECES, n * step)),
         out_shape=(
             jax.ShapeDtypeStruct((tiles, 8, 128), bf16),
             jax.ShapeDtypeStruct((shard,), f32),
@@ -837,10 +822,7 @@
         in_specs=[vmem] * 4,
         out_specs=(anywhere, anywhere, anywhere),
         scratch_shapes=[
-            pltpu.VMEM((shard,), f32),
-            pltpu.VMEM((shard,), f32),
-            dma((PIECES + 1,)),
-            dma((2,)),
+            dma((PIECES + 3,)),
         ],
         compiler_params=pltpu.CompilerParams(vmem_limit_bytes=16 * 2**20),
     )(ags.reshape(n * step, 8, 128), age, nmw, nvw)

time: 39.9 us -> 40 us (level)
  no operation moved by 1% of the time
where the time goes in v8:
time: 40 us; the launch traced here: 39.9 us
  Pallas kernels  39.3 us (98%)
  between operations  0.64 us (2%)
    pallas_call x1, Pallas kernels, windowed(): pl.pallas_call(functools.partial(kernel, plan), out_shape=(pltpu.VMEM((n,...  37.9 us
    pallas_call x1, Pallas kernels, windowed(): pl.pallas_call(functools.partial(finish, (n * step // PIECES, n * step)),...  1.34 us

profile of v8, /device:TPU:0, one launch (start us, length us, event | category | flops | bytes accessed | tf_op | source)
XLA Modules:
  0.0 39.9 jit_solution(12776133520123293062)
XLA Ops:
  0.6 37.9 %shard_map.85 = (bf16[32,26,8,128]{3,2,1,0:T(8,128)(2,1)S(1)}, bf16[1,8,128]{2,1,0:T(8,128)(2,1)S(1)}, f32[26656]{0:T(1024)S(1)}, f32[26656]{0:T(1024)S(1)}) custom-call(bf16[1,1,852992]{2,1,0:T(2,128)(2,1)} %grads_ref.1, f32[26656]{0:T(1024)} %m_ref.1, f32[26656]{0:T(1024)} %v_ref.1, s32[6]{0:T(128)} %offsets_in.1, s32[6]{0:T(128)} %sizes_in.1, s32[6]{0:T(128)} %skip_in.1), custom_call_target="tpu_custom_call" | custom-call | tf_op jit(solution)/shard_map/pallas_call | solution.py:734
  38.6 1.3 %shard_map.86 = (bf16[833,8,128]{2,1,0:T(8,128)(2,1)}, f32[26656]{0:T(1024)}, f32[26656]{0:T(1024)}) custom-call(bf16[832,8,128]{2,1,0:T(8,128)(2,1)S(1)} %bitcast.2, bf16[1,8,128]{2,1,0:T(8,128)(2,1)S(1)} %get-tuple-element.11.age, f32[26656]{0:T(1024)S(1)} %get-tuple-element.12.nm, f32[26656]{0:T(1024)S(1)} %get-tuple-element.13.nv), custom_call_target="tpu_custom_call" | custom-call | tf_op jit(solution)/shard_map/pallas_call | solution.py:815
